TPU v7x, 32 devices: a whole 2x2x4 slice. The times are simulated.
32 devices in a mesh: mem: 8 (over z, x), rep: 4 (over y, core).
Axes of the slice: x: 2, y: 2, z: 4, core: 2. Of those that a mesh axis runs over, the one named last changes fastest.
Arguments:
- memory: float32 [8192, 172], P('mem'), may hold values from -6 to 6
- node_slot: int32 [8192], replicated, may hold values from 0 to 8191, as said below
- event_nodes: int32 [2, 4096, 33], P(None, ('mem', 'rep')), may hold values from 0 to 8191, as said below
- event_times: int32 [2, 4096], P(None, ('mem', 'rep')), may hold values from 0 to 999
- valid_mask: int32 [2, 4096], P(None, ('mem', 'rep')), may hold values 0 or 1
- time_freq: float32 [100], replicated, may hold values from 0.001 to 1
- time_phase: float32 [100], replicated, may hold values from -3.140625 to 3.140625
- gru_input: bfloat16 [444, 516], replicated, may hold values from -0.25 to 0.25
- gru_hidden: bfloat16 [172, 516], replicated, may hold values from -0.4375 to 0.4375
- gru_in_bias: float32 [516], replicated, may hold values from -3 to 3
- gru_hid_bias: float32 [516], replicated, may hold values from -3 to 3
- w_self: float32 [172, 100], replicated, may hold values from -0.4375 to 0.4375
- w_nbr: float32 [172, 100], replicated, may hold values from -0.4375 to 0.4375
- b_embed: float32 [100], replicated, may hold values from -3 to 3
- w_dec1: float32 [200, 100], replicated, may hold values from -0.4375 to 0.4375
- b_dec1: float32 [100], replicated, may hold values from -3 to 3
- w_dec2: float32 [100], replicated, may hold values from -0.625 to 0.625
- b_dec2: float32 [1], replicated, may hold values from -3 to 3
Outputs:
- memory_out: float32 [8192, 172], P('mem')
- batch_losses: float32 [2], replicated
- w_self_out: float32 [172, 100], replicated
- w_nbr_out: float32 [172, 100], replicated
- b_embed_out: float32 [100], replicated
- w_dec1_out: float32 [200, 100], replicated
- b_dec1_out: float32 [100], replicated
- w_dec2_out: float32 [100], replicated
- b_dec2_out: float32 [1], replicated
Inputs may be any that keep to these rules, and one draw needn't show every extreme that they name: A permutation: node n's memory is row node_slot[n] of memory. `event_nodes`: columns 0, 1, 2 of an event are its source, destination and negative node; column 3 + r * 10 + k is neighbour k of column r. Among one device's events of one batch, the nodes of columns 0 and 1 whose slots lie in one block of 1024 slots are at most 64, and those of the other columns at most 620; in every such group of events one block of slots receives exactly 64 and 620.
All inputs are finite; a program needn't handle non-finite values. No bound on the sum of `valid_mask` on one device may be relied on, other than what follows from the above.
Results may differ from a plain program's by a relative error of at most 0.002.
Values may be sent and summed in bfloat16 or wider, within the bound.
A program may use at most 128 MiB of HBM per device.

v0:
```python
import jax
import jax.numpy as jnp
from jax import lax
from jax.sharding import PartitionSpec as P

step_size = 4.0


def block_loss(current, own_rows, beside_sum, neighbours, valid_part):
    w_self, w_nbr, b_embed, w_dec1, b_dec1, w_dec2, b_dec2 = current
    num_events = own_rows.shape[0] // 3
    direct = jnp.dot(own_rows, w_self.astype(jnp.bfloat16), preferred_element_type=jnp.float32)
    spread = jnp.dot(
        beside_sum,
        w_nbr.astype(jnp.bfloat16).astype(jnp.float32),
        precision=lax.Precision.HIGHEST,
    )
    hidden = jnp.tanh(direct + spread * (1.0 / neighbours) + b_embed).astype(jnp.bfloat16)
    first = hidden[:num_events]
    paired = jnp.concatenate(
        [jnp.concatenate([first, first], 0), hidden[num_events:]],
        1,
    )
    inner_act = jax.nn.relu(
        jnp.dot(paired, w_dec1.astype(jnp.bfloat16), preferred_element_type=jnp.float32) + b_dec1
    )
    logits = jnp.sum(inner_act * w_dec2, 1) + b_dec2[0]
    weights = valid_part.astype(jnp.float32)
    sign_flip = jnp.concatenate(
        [-jnp.ones((num_events,), jnp.float32), jnp.ones((num_events,), jnp.float32)]
    )
    return jnp.sum(jax.nn.softplus(sign_flip * logits) * jnp.concatenate([weights, weights]))


def normalized_step(params, gradients):
    total = jnp.zeros((), jnp.float32)
    for grad_part in gradients:
        total = total + jnp.sum(grad_part * grad_part)
    factor = step_size / (jnp.sqrt(total) + 1e-06)
    return tuple((value - factor * grad_part for value, grad_part in zip(params, gradients)))


def memory_update(
    mean_rest, state_bf, old_state, gru_input, gru_hidden, gru_in_bias, gru_hid_bias
):
    row_width = old_state.shape[1]
    from_input = (
        jnp.dot(state_bf, gru_input[:row_width], preferred_element_type=jnp.float32)
        + jnp.dot(mean_rest, gru_input[row_width:], preferred_element_type=jnp.float32)
        + gru_in_bias
    )
    from_state = jnp.dot(state_bf, gru_hidden, preferred_element_type=jnp.float32) + gru_hid_bias
    reset = jax.nn.sigmoid(from_input[:, :row_width] + from_state[:, :row_width])
    update = jax.nn.sigmoid(
        from_input[:, row_width : 2 * row_width] + from_state[:, row_width : 2 * row_width]
    )
    candidate = jnp.tanh(from_input[:, 2 * row_width :] + reset * from_state[:, 2 * row_width :])
    return (1.0 - update) * candidate + update * old_state


def look_up(table, ids):
    width = 128
    groups = table.shape[0] // width
    grid = table.reshape(groups, width)
    digits = jnp.concatenate([grid >> 8, grid & 255], 1).astype(jnp.bfloat16)
    pick = ((ids // width)[..., None] == jnp.arange(groups, dtype=jnp.int32)).astype(jnp.bfloat16)
    rows = jnp.dot(pick, digits, preferred_element_type=jnp.float32)
    here = (ids % width)[..., None] == jnp.arange(width, dtype=jnp.int32)
    both = jnp.where(here, rows[..., :width] * 256.0 + rows[..., width:], 0.0)
    return jnp.sum(both, -1).astype(jnp.int32)


def sum_everywhere(gradients, loss_local, count_local, devices):
    g_self, g_nbr, g_embed, g_dec1, g_bias1, g_dec2, g_bias2 = gradients
    width = g_self.shape[1]
    scalars = jnp.concatenate([g_bias2, loss_local[None], count_local[None]])
    scalars = jnp.pad(scalars, (0, width - scalars.shape[0]))
    table = jnp.concatenate(
        [g_self, g_nbr, g_dec1, jnp.stack([g_embed, g_bias1, g_dec2, scalars])], 0
    )
    used = table.shape[0]
    share = -(-used // (devices * 8)) * 8
    table = jnp.pad(table, ((0, share * devices - used), (0, 0))).reshape(devices, share, width)
    parts = lax.all_to_all(table, ("mem", "rep"), split_axis=0, concat_axis=0, tiled=True)
    total = lax.all_gather(jnp.sum(parts, 0), ("mem", "rep"), axis=0, tiled=True)
    n_self, n_nbr, n_dec1 = g_self.shape[0], g_nbr.shape[0], g_dec1.shape[0]
    at = n_self + n_nbr + n_dec1
    return (
        (
            total[:n_self],
            total[n_self : n_self + n_nbr],
            total[at],
            total[n_self + n_nbr : at],
            total[at + 1],
            total[at + 2],
            total[at + 3, :1],
        ),
        total[at + 3, 1],
        total[at + 3, 2],
    )


def place_rows(owner_ids, owners, stride, offset):
    length = owner_ids.shape[0]
    width = 128
    groups = -(-length // width)
    padded_ids = owner_ids.reshape(groups, width)
    one_hot = (padded_ids[:, :, None] == jnp.arange(owners, dtype=jnp.int32)[None, None, :]).astype(
        jnp.float32
    )
    lower = (
        jnp.arange(width, dtype=jnp.int32)[:, None] > jnp.arange(width, dtype=jnp.int32)[None, :]
    ).astype(jnp.float32)
    within = jnp.einsum("ij,gjo->gio", lower, one_hot, precision=lax.Precision.HIGHEST)
    totals = jnp.sum(one_hot, 1)
    starts = jnp.cumsum(totals, 0) - totals
    before = jnp.sum((within + starts[:, None, :]) * one_hot, 2).reshape(-1)
    return owner_ids * stride + offset + before.astype(jnp.int32)


def body(
    memory,
    node_slot,
    event_nodes,
    event_times,
    valid_mask,
    time_freq,
    time_phase,
    gru_input,
    gru_hidden,
    gru_in_bias,
    gru_hid_bias,
    w_self,
    w_nbr,
    b_embed,
    w_dec1,
    b_dec1,
    w_dec2,
    b_dec2,
):
    owners = lax.axis_size("mem")
    devices = owners * lax.axis_size("rep")
    node_dev, row_width = memory.shape
    batches, events, columns = event_nodes.shape
    neighbours = (columns - 3) // 3
    cap_pair = 2 * events // owners * 2
    params = (w_self, w_nbr, b_embed, w_dec1, b_dec1, w_dec2, b_dec2)
    losses = []
    all_slots = look_up(node_slot, event_nodes.transpose(0, 2, 1))
    for batch_index in range(batches):
        slot_ids = all_slots[batch_index]
        memory_bf = memory.astype(jnp.bfloat16)
        whole_bf = lax.all_gather(memory_bf, "mem", axis=0, tiled=True)
        fetched = jnp.take(whole_bf, slot_ids.reshape(-1), axis=0, mode="clip")
        own_rows = fetched[: 3 * events]
        beside = fetched[3 * events :].reshape(3, neighbours, events, row_width)
        beside_sum = jnp.sum(beside.astype(jnp.float32), 1).reshape(3 * events, row_width)

        pair_slots = slot_ids[:2].reshape(-1)
        pair_at = place_rows(pair_slots // node_dev, owners, cap_pair, 0)
        offsets = (pair_slots % node_dev).astype(jnp.int32)
        time_code = jnp.cos(
            event_times[batch_index].astype(jnp.float32)[:, None] * time_freq + time_phase
        ).astype(jnp.bfloat16)
        marks = jnp.stack([jnp.ones_like(offsets), offsets // 128, offsets % 128], 1)
        partners = jnp.concatenate([own_rows[events : 2 * events], own_rows[:events]], 0)
        letters = jnp.concatenate(
            [partners, jnp.concatenate([time_code, time_code], 0), marks.astype(jnp.bfloat16)], 1
        )
        seats = jnp.arange(owners * cap_pair, dtype=jnp.int32)[:, None] == pair_at[None, :]
        parcel = jnp.dot(
            seats.astype(jnp.bfloat16), letters, preferred_element_type=jnp.float32
        ).astype(jnp.bfloat16)
        parcel = parcel.reshape(owners, cap_pair, letters.shape[1])
        parcel = lax.all_to_all(parcel, "mem", split_axis=0, concat_axis=0, tiled=True)
        every_parcel = lax.all_gather(parcel, "rep", axis=0, tiled=True)
        every_parcel = every_parcel.reshape(-1, letters.shape[1])
        digits = every_parcel[:, -2:].astype(jnp.int32)
        target = digits[:, 0] * 128 + digits[:, 1]
        matches = jnp.arange(node_dev, dtype=jnp.int32)[:, None] == target[None, :]
        summed = jnp.dot(
            matches.astype(jnp.bfloat16), every_parcel, preferred_element_type=jnp.float32
        )
        counts = summed[:, -3:-2]
        mean_rest = (summed[:, :-3] / jnp.maximum(counts, 1.0)).astype(jnp.bfloat16)
        fresh = memory_update(
            mean_rest, memory_bf, memory, gru_input, gru_hidden, gru_in_bias, gru_hid_bias
        )
        memory = jnp.where(counts > 0, fresh, memory)

        valid_part = valid_mask[batch_index]
        loss_local, pullback = jax.vjp(
            lambda current: block_loss(current, own_rows, beside_sum, neighbours, valid_part),
            params,
        )
        gradients = pullback(jnp.ones_like(loss_local))[0]
        count_local = jnp.sum(valid_part.astype(jnp.float32))
        gradients, loss_total, count_total = sum_everywhere(
            gradients, loss_local, count_local, devices
        )
        params = normalized_step(params, gradients)
        losses.append(loss_total / jnp.maximum(count_total, 1.0))
    return (
        memory,
        jnp.stack(losses),
        params[0],
        params[1],
        params[2],
        params[3],
        params[4],
        params[5],
        params[6],
    )


def solution(mesh):
    return jax.shard_map(
        body,
        mesh=mesh,
        in_specs=(
            P("mem", None),
            P(),
            P(None, ("mem", "rep"), None),
            P(None, ("mem", "rep")),
            P(None, ("mem", "rep")),
            P(),
            P(),
            P(),
            P(),
            P(),
            P(),
            P(),
            P(),
            P(),
            P(),
            P(),
            P(),
            P(),
        ),
        out_specs=(P("mem", None), P(), P(), P(), P(), P(), P(), P(), P()),
        check_vma=False,
    )
```

profile of v0, /device:TPU:0, one launch (start us, length us, event | category | flops | bytes accessed | tf_op | source)
XLA Modules:
  0.0 355.3 jit_solution(9725286313087995322)
XLA Ops:
  7.2 2.2 copy.57
  12.5 3.1 fusion.3
  18.3 67.9 %all-gather.5.cloned.1.call-done = bf16[8192,172]{1,0:T(8,128)(2,1)} async-done(((bf16[1024,172]{1,0:T(8,128)(2,1)}), bf16[8192,172]{1,0:T(8,128)(2,1)}) %all-gather.5.cloned.1.call-update) | async-done | bytes 2818064 | tf_op jit(solution)/shard_map/all_gather | solution.py:153
  86.3 12.3 %gather_fusion = bf16[4224,172]{1,0:T(8,128)(2,1)S(1)} fusion(bf16[8192,172]{1,0:T(8,128)(2,1)} %all-gather.5.cloned.1.call-done, s32[5120]{0:T(1024)S(1)} %pad_clamp_fusion.1), kind=kCustom, calls=%fused_computation | custom fusion | bytes 2923008 | tf_op jit(solution)/shard_map/jit(_take)/gather | solution.py:154
  102.0 15.1 %all_to_all.20 = bf16[8,64,275]{2,1,0:T(8,128)(2,1)} all-to-all(bf16[8,64,275]{2,1,0:T(8,128)(2,1)S(1)} %bitcast.175), channel_id=1, replica_groups=mesh['mem'=8,'rep'=4] {'mem'}, dimensions={0} | all-to-all | bytes 563200 | tf_op jit(solution)/shard_map/all_to_all | solution.py:175
  117.4 1.8 convolution_add_fusion
  119.2 1.8 fusion.66
  121.0 14.4 %all-gather.7.cloned.1.call-done = bf16[32,64,275]{2,1,0:T(8,128)(2,1)} async-done(((bf16[8,64,275]{2,1,0:T(8,128)(2,1)}), bf16[32,64,275]{2,1,0:T(8,128)(2,1)}) %all-gather.7.cloned.1.call-update) | async-done | bytes 1126416 | tf_op jit(solution)/shard_map/all_gather | solution.py:176
  137.6 2.0 fusion.1
  141.4 1.6 fusion.145
  147.8 2.0 fusion.127
  152.3 4.6 %all-to-all-start.2 = ((f32[32,24,100]{2,1,0:T(8,128)}), f32[32,24,100]{2,1,0:T(8,128)S(1)}, u32[]{:S(2)}, u32[]{:S(2)}) async-start(f32[32,24,100]{2,1,0:T(8,128)} %bitcast.37), calls=%async_computation.2 | async-start | bytes 786432 | tf_op jit(solution)/shard_map/all_to_all | solution.py:84
  157.9 18.0 %all-to-all-done.2 = f32[32,24,100]{2,1,0:T(8,128)S(1)} async-done(((f32[32,24,100]{2,1,0:T(8,128)}), f32[32,24,100]{2,1,0:T(8,128)S(1)}, u32[]{:S(2)}, u32[]{:S(2)}) %all-to-all-start.2) | async-done | bytes 307232 | tf_op jit(solution)/shard_map/all_to_all | solution.py:84
  175.9 42.3 %all_gather.22 = f32[768,100]{1,0:T(8,128)S(1)} all-gather(f32[24,100]{1,0:T(8,128)S(1)} %reduce_sum.364), channel_id=1, replica_groups=mesh['mem'=8,'rep'=4] {'mem','rep'}, dimensions={0}, use_global_device_ids=true | all-gather | bytes 316800 | tf_op jit(solution)/shard_map/all_gather | solution.py:85
  226.7 5.8 %copy.62 = bf16[8192,172]{1,0:T(8,128)(2,1)} copy(bf16[8192,172]{0,1:T(8,128)(2,1)} %all-gather.9.cloned.1.call-done) | data formatting | bytes 5636096 | tf_op jit(solution)/shard_map/all_gather | solution.py:153
  232.5 12.3 %gather_fusion.1 = bf16[4224,172]{1,0:T(8,128)(2,1)S(1)} fusion(bf16[8192,172]{1,0:T(8,128)(2,1)} %copy.62, s32[5120]{0:T(1024)S(1)} %pad_clamp_fusion), kind=kCustom, calls=%fused_computation.1 | custom fusion | bytes 2923008 | tf_op jit(solution)/shard_map/jit(_take)/gather | solution.py:154
  250.7 1.7 concatenate.72
  254.6 4.2 %all-to-all-start.1 = ((bf16[8,64,275]{2,1,0:T(8,128)(2,1)}), bf16[8,64,275]{2,1,0:T(8,128)(2,1)}, u32[]{:S(2)}, u32[]{:S(2)}) async-start(bf16[8,64,275]{2,1,0:T(8,128)(2,1)} %bitcast.174), calls=%async_computation.1 | async-start | bytes 786432 | tf_op jit(solution)/shard_map/all_to_all | solution.py:175
  259.9 2.0 fusion.126
  261.9 1.8 fusion.15
  263.7 1.8 fusion.17
  265.5 2.0 concatenate.86
  268.3 3.0 all-to-all-done.1
  271.3 2.7 all-to-all-start.3
  275.2 1.8 fusion.64
  277.6 9.7 %all-to-all-done.3 = f32[32,24,100]{2,1,0:T(8,128)S(1)} async-done(((f32[32,24,100]{2,1,0:T(8,128)}), f32[32,24,100]{2,1,0:T(8,128)S(1)}, u32[]{:S(2)}, u32[]{:S(2)}) %all-to-all-start.3) | async-done | bytes 307232 | tf_op jit(solution)/shard_map/all_to_all | solution.py:84
  287.3 39.6 %all_gather.23 = f32[768,100]{1,0:T(8,128)S(1)} all-gather(f32[24,100]{1,0:T(8,128)S(1)} %reduce_sum.380), channel_id=1, replica_groups=mesh['mem'=8,'rep'=4] {'mem','rep'}, dimensions={0}, use_global_device_ids=true | all-gather | bytes 316800 | tf_op jit(solution)/shard_map/all_gather | solution.py:85
  337.7 1.6 multiply_subtract_fusion
  339.3 1.6 multiply_subtract_fusion.2
  340.9 1.4 slice_convert_fusion
  343.0 2.0 fusion
  346.2 1.4 fusion.34
  (183 shorter events, 38.8 us)
Async XLA Ops:
  7.2 110.2 %copy-start = (bf16[172,516]{1,0:T(8,128)(2,1)S(1)}, bf16[172,516]{1,0:T(8,128)(2,1)}, u32[]{:S(2)}) copy-start(bf16[172,516]{1,0:T(8,128)(2,1)} %param.27) | copy-start | bytes 532516
  7.2 79.1 %all-gather.5.cloned.1.call-start = ((), (), s32[]{:S(2)}) async-start(), calls=%async_computation.4 | async-start | bytes 4718592 | tf_op jit(solution)/shard_map/all_gather | solution.py:153
  9.4 126.0 %all-gather.7.cloned.1.call-start = ((), (), s32[]{:S(2)}) async-start(), calls=%async_computation.5 | async-start | bytes 1966080 | tf_op jit(solution)/shard_map/all_gather | solution.py:176
  12.5 3.9 %copy-start.33 = (s32[2,128]{1,0:T(2,128)S(1)}, s32[2,128]{1,0:T(2,128)}, u32[]{:S(2)}) copy-start(s32[2,128]{1,0:T(2,128)} %param.22) | copy-start | bytes 3076
  12.5 3.9 %copy-start.34 = (f32[100]{0:T(128)S(1)}, f32[100]{0:T(128)}, u32[]{:S(2)}) copy-start(f32[100]{0:T(128)} %param.25) | copy-start | bytes 1204
  12.5 3.9 %copy-start.35 = (f32[100]{0:T(128)S(1)}, f32[100]{0:T(128)}, u32[]{:S(2)}) copy-start(f32[100]{0:T(128)} %param.24) | copy-start | bytes 1204
  98.6 18.8 %copy-start.2 = (bf16[1024,172]{1,0:T(8,128)(2,1)S(1)}, bf16[1024,172]{1,0:T(8,128)(2,1)}, u32[]{:S(2)}) copy-start(bf16[1024,172]{1,0:T(8,128)(2,1)} %copy.57) | copy-start | bytes 1056772
  98.6 18.8 %copy-start.17 = (f32[516]{0:T(1024)S(1)}, f32[516]{0:T(1024)}, u32[]{:S(2)}) copy-start(f32[516]{0:T(1024)} %param.29) | copy-start | bytes 6196
  117.1 109.6 %all-gather.9.cloned.1.call-start = ((), (), s32[]{:S(2)}) async-start(), calls=%async_computation.6 | async-start | bytes 3244032 | tf_op jit(solution)/shard_map/all_gather | solution.py:153
  135.5 2.1 copy-start.16
  137.5 2.1 copy-start.6
  137.5 2.1 copy-start.12
  137.5 2.1 copy-start.37
  141.4 2.3 copy-start.26
  152.3 23.5 %all-to-all-start.2 = ((f32[32,24,100]{2,1,0:T(8,128)}), f32[32,24,100]{2,1,0:T(8,128)S(1)}, u32[]{:S(2)}, u32[]{:S(2)}) async-start(f32[32,24,100]{2,1,0:T(8,128)} %bitcast.37), calls=%async_computation.2 | async-start | bytes 786432 | tf_op jit(solution)/shard_map/all_to_all | solution.py:84
  226.6 19.0 %copy-start.22 = (f32[100]{0:T(128)}, f32[100]{0:T(128)S(1)}, u32[]{:S(2)}) copy-start(f32[100]{0:T(128)S(1)} %get-tuple-element.57) | copy-start | bytes 1204
  226.6 20.0 %copy-start.28 = (f32[100]{0:T(128)}, f32[100]{0:T(128)S(1)}, u32[]{:S(2)}) copy-start(f32[100]{0:T(128)S(1)} %get-tuple-element.58) | copy-start | bytes 1204
  226.6 23.1 %copy-start.20 = (f32[100]{0:T(128)}, f32[100]{0:T(128)S(1)}, u32[]{:S(2)}) copy-start(f32[100]{0:T(128)S(1)} %get-tuple-element.56) | copy-start | bytes 1204
  250.7 14.8 %copy-start.31 = (f32[100]{0:T(128)S(1)}, f32[100]{0:T(128)}, u32[]{:S(2)}) copy-start(f32[100]{0:T(128)} %get-tuple-element.29) | copy-start | bytes 1204
  250.7 14.8 %copy-start.32 = (f32[100]{0:T(128)S(1)}, f32[100]{0:T(128)}, u32[]{:S(2)}) copy-start(f32[100]{0:T(128)} %get-tuple-element.30) | copy-start | bytes 1204
  254.6 20.6 %copy-start.3 = (bf16[1024,172]{0,1:T(8,128)(2,1)S(1)}, bf16[1024,172]{0,1:T(8,128)(2,1)}, u32[]{:S(2)}) copy-start(bf16[1024,172]{0,1:T(8,128)(2,1)} %get-tuple-element.39) | copy-start | bytes 1056772
  254.6 16.7 %all-to-all-start.1 = ((bf16[8,64,275]{2,1,0:T(8,128)(2,1)}), bf16[8,64,275]{2,1,0:T(8,128)(2,1)}, u32[]{:S(2)}, u32[]{:S(2)}) async-start(bf16[8,64,275]{2,1,0:T(8,128)(2,1)} %bitcast.174), calls=%async_computation.1 | async-start | bytes 786432 | tf_op jit(solution)/shard_map/all_to_all | solution.py:175
  263.7 11.5 %copy-start.13 = (bf16[444,516]{0,1:T(8,128)(2,1)S(1)}, bf16[444,516]{0,1:T(8,128)(2,1)}, u32[]{:S(2)}) copy-start(bf16[444,516]{0,1:T(8,128)(2,1)} %param.26) | copy-start | bytes 1374628
  268.3 8.8 %copy-start.18 = (f32[516]{0:T(1024)S(1)}, f32[516]{0:T(1024)}, u32[]{:S(2)}) copy-start(f32[516]{0:T(1024)} %param.29) | copy-start | bytes 6196
  271.3 16.0 %all-to-all-start.3 = ((f32[32,24,100]{2,1,0:T(8,128)}), f32[32,24,100]{2,1,0:T(8,128)S(1)}, u32[]{:S(2)}, u32[]{:S(2)}) async-start(f32[32,24,100]{2,1,0:T(8,128)} %bitcast.56), calls=%async_computation.3 | async-start | bytes 786432 | tf_op jit(solution)/shard_map/all_to_all | solution.py:84
  274.0 66.9 %all-gather.11.cloned.1.call-start = ((), (), s32[]{:S(2)}) async-start(), calls=%async_computation.7 | async-start | bytes 1966080 | tf_op jit(solution)/shard_map/all_gather | solution.py:176
  277.0 60.2 %copy-start.21 = (f32[100]{0:T(128)S(1)}, f32[100]{0:T(128)}, u32[]{:S(2)}) copy-start(f32[100]{0:T(128)} %copy-done.20) | copy-start | bytes 1204
  277.0 60.2 %copy-start.23 = (f32[100]{0:T(128)S(1)}, f32[100]{0:T(128)}, u32[]{:S(2)}) copy-start(f32[100]{0:T(128)} %copy-done.22) | copy-start | bytes 1204
  277.0 60.2 %copy-start.29 = (f32[100]{0:T(128)S(1)}, f32[100]{0:T(128)}, u32[]{:S(2)}) copy-start(f32[100]{0:T(128)} %copy-done.28) | copy-start | bytes 1204
  340.9 2.1 copy-start.15
  343.0 2.1 copy-start.7
  343.0 2.1 copy-start.14
  (14 other events, 21.1 us)
Sparse Core Ops, SparseCore 0:
  10.7 75.5 all-gather.4
  117.2 18.1 all-gather.6
  143.1 65.9 all-gather.8
  277.2 21.7 all-gather.10
where the time goes:
time: 357 us; the launch traced here: 355 us
  waiting for transfers between devices  113 us (32%)
  blocking collectives  97 us (27%)
  local copies, waits for them, and re-layouts  45.8 us (13%)
  other arithmetic  32.9 us (9%)
  between operations  30.8 us (9%)
  matrix products  23.9 us (7%)
  starting transfers between devices  11.9 us (3%)
    all_gather x2, blocking collectives, sum_everywhere(): lax.all_gather(jnp.sum(parts, 0), ('mem', 'rep'), axis=0, tiled=True)  81.9 us
    all_gather x2, waiting for transfers between devices, body(): whole_bf = lax.all_gather(memory_bf, 'mem', axis=0, tiled=True)  67.9 us
    all_to_all x2, waiting for transfers between devices, sum_everywhere(): lax.all_to_all(table, ('mem', 'rep'), split_axis=0, concat_axis=0, tiled=...  27.7 us
    gather x2, local copies, waits for them, and re-layouts, body(): fetched = jnp.take(whole_bf, slot_ids.reshape(-1), axis=0, mode='clip')  24.7 us
    all_to_all x1, blocking collectives, body(): lax.all_to_all(parcel, 'mem', split_axis=0, concat_axis=0, tiled=True)  15.1 us
    all_gather x2, waiting for transfers between devices, body(): every_parcel = lax.all_gather(parcel, 'rep', axis=0, tiled=True)  14.4 us
    all_to_all x2, starting transfers between devices, sum_everywhere(): lax.all_to_all(table, ('mem', 'rep'), split_axis=0, concat_axis=0, tiled=...  7.3 us
  transfers between devices with their start and end apart: 7, of which 5 were waited for; matrix products, arithmetic and copies ran while one was open for 12% of the time, Pallas kernels for 0%

commit v1 on v0

--- a/solution.py
+++ b/solution.py
@@ -1,9 +1,837 @@
+import functools
+
 import jax
 import jax.numpy as jnp
 from jax import lax
+from jax.experimental import pallas as pl
+from jax.experimental.pallas import tpu as pltpu
 from jax.sharding import PartitionSpec as P
 
 step_size = 4.0
+LANES = 128
+TIMES = 1000
+MESH_ID = pl.DeviceIdType.MESH
+BF = jnp.bfloat16
+F32 = jnp.float32
+HI = lax.Precision.HIGHEST
+
+
+def vmem(count):
+    return [pl.BlockSpec(memory_space=pltpu.VMEM)] * count
+
+
+def dot(a, b, precision=None):
+    return lax.dot_general(
+        a, b, (((1,), (0,)), ((), ())), precision=precision, preferred_element_type=F32
+    )
+
+
+def dot_tn(a, b, precision=None):
+    return lax.dot_general(
+        a, b, (((0,), (0,)), ((), ())), precision=precision, preferred_element_type=F32
+    )
+
+
+def dot_nt(a, b, precision=None):
+    return lax.dot_general(
+        a, b, (((1,), (1,)), ((), ())), precision=precision, preferred_element_type=F32
+    )
+
+
+def iota(shape, axis):
+    return lax.broadcasted_iota(jnp.int32, shape, axis)
+
+
+def pad_lanes(x):
+    return jnp.concatenate([x, jnp.zeros((x.shape[0], LANES - x.shape[1]), x.dtype)], 1)
+
+
+def pad_rows(x, rows):
+    return jnp.concatenate([x, jnp.zeros((rows - x.shape[0], x.shape[1]), x.dtype)], 0)
+
+
+def lists_kernel(owners, node_dev, cap, width, slot_ref, pair_ref, time_ref, freq_ref, phase_ref, lists_ref, codes_ref):
+    groups = slot_ref.shape[0]
+    ids = pair_ref[...]
+    letters = ids.shape[1]
+    per_batch = letters // 2
+    grid = slot_ref[...]
+    digits = jnp.concatenate([grid >> 8, grid & 255], 1).astype(F32).astype(BF)
+    group_hot = jnp.where(iota((groups, letters), 0) == (ids >> 7), 1.0, 0.0).astype(BF)
+    found = dot_tn(digits, group_hot)
+    here = iota((LANES, letters), 0) == (ids & 127)
+    slots_f = jnp.sum(jnp.where(here, found[:LANES] * 256.0 + found[LANES:], 0.0), 0, keepdims=True)
+    slots = slots_f.astype(jnp.int32)
+    events = per_batch // 2
+    partners = jnp.concatenate(
+        [
+            slots[:, events : 2 * events],
+            slots[:, :events],
+            slots[:, 3 * events :],
+            slots[:, 2 * events : 3 * events],
+        ],
+        1,
+    )
+    owner = slots // node_dev
+    offset = slots - owner * node_dev
+    owner_hot = jnp.where(iota((owners, letters), 0) == owner, 1.0, 0.0)
+    earlier = jnp.where(
+        iota((per_batch, per_batch), 0) < iota((per_batch, per_batch), 1), 1.0, 0.0
+    ).astype(BF)
+    hot_bf = owner_hot.astype(BF)
+    before = jnp.concatenate(
+        [dot(hot_bf[:, :per_batch], earlier), dot(hot_bf[:, per_batch:], earlier)], 1
+    )
+    rank = jnp.sum(before * owner_hot, 0, keepdims=True).astype(jnp.int32)
+    batch = iota((1, letters), 1) // per_batch
+    seat = owner * (2 * cap) + batch * cap + rank
+    times = time_ref[...]
+    values = jnp.concatenate(
+        [
+            offset >> 8, offset & 255, partners >> 8, partners & 255,
+            times >> 8, times & 255, jnp.ones_like(times), jnp.zeros_like(times),
+        ],
+        0,
+    ).astype(F32).astype(BF)
+    for o in range(owners):
+        seats = jnp.where(iota((2 * cap, letters), 0) + o * 2 * cap == seat, 1.0, 0.0).astype(BF)
+        placed = dot_nt(values, seats)
+        taken = placed[6:7] > 0.5
+        rows = [
+            jnp.where(taken, placed[0:1] * 256.0 + placed[1:2], float(node_dev)),
+            placed[2:3] * 256.0 + placed[3:4],
+            placed[4:5] * 256.0 + placed[5:6],
+        ]
+        lists_ref[o] = jnp.concatenate(rows + [jnp.zeros((5, 2 * cap), F32)], 0).astype(jnp.int32)
+    stamps = iota(codes_ref.shape, 0).astype(F32)
+    code = jnp.cos(stamps * freq_ref[...] + phase_ref[...])
+    lane = iota(codes_ref.shape, 1)
+    code = jnp.where(lane < width, code, jnp.where(lane == width, 1.0, 0.0))
+    codes_ref[...] = code.astype(BF)
+
+
+def peer(index, reps):
+    return (index // reps, lax.rem(index, reps))
+
+
+def enter(devices, reps, me):
+    barrier = pltpu.get_barrier_semaphore()
+
+    def greet(k, carry):
+        pl.semaphore_signal(
+            barrier, inc=1, device_id=peer(lax.rem(me + k, devices), reps), device_id_type=MESH_ID
+        )
+        return carry
+
+    lax.fori_loop(1, devices, greet, 0)
+    pl.semaphore_wait(barrier, devices - 1)
+
+
+class Gather:
+    def __init__(self, owners, own_ref, table_ref, send_sem, recv_sem, local_sem):
+        self.outer = owners // 2
+        mem = lax.axis_index("mem")
+        rep = lax.axis_index("rep")
+        self.a, self.b = mem // 2, lax.rem(mem, 2)
+        self.u, self.c = rep // 2, lax.rem(rep, 2)
+        self.mem, self.rep = mem, rep
+        self.own, self.table = own_ref, table_ref
+        self.send_sem, self.recv_sem = send_sem, recv_sem
+        self.local = pltpu.make_async_copy(own_ref, table_ref.at[mem], local_sem)
+        self.sent = []
+
+    def push(self, shard, block, target, from_own=False):
+        src = self.own.at[block] if from_own else self.table.at[shard, block]
+        copy = pltpu.make_async_remote_copy(
+            src_ref=src,
+            dst_ref=self.table.at[shard, block],
+            send_sem=self.send_sem.at[len(self.sent)],
+            recv_sem=self.recv_sem.at[shard, block],
+            device_id=target,
+            device_id_type=MESH_ID,
+        )
+        copy.start()
+        self.sent.append(copy)
+
+    def arrived(self, shard, block):
+        pltpu.make_async_copy(
+            self.table.at[shard, block], self.table.at[shard, block], self.recv_sem.at[shard, block]
+        ).wait()
+
+    def begin(self):
+        self.local.start()
+        a, b, u, c, rep = self.a, self.b, self.u, self.c, self.rep
+        mine = (3 * c + u, 3 * c + 2)
+        self.mine = mine
+        for block in mine:
+            self.push(self.mem, block, (2 * a + 1 - b, rep), True)
+            for d in range(1, self.outer):
+                self.push(self.mem, block, (2 * lax.rem(a + d, self.outer) + b, rep), True)
+
+    def steps(self):
+        a, b, u, c, rep, mem = self.a, self.b, self.u, self.c, self.rep, self.mem
+        beside_x = (2 * a + 1 - b, rep)
+        beside_y = (mem, 2 * (1 - u) + c)
+        beside_core = (mem, 2 * u + 1 - c)
+        order = [(0, 1)]
+        for d in range(1, self.outer):
+            order.append((d, 0))
+        for d in range(1, self.outer):
+            order.append((d, 1))
+        shards = []
+        for d, other in order:
+            shards.append((2 * lax.rem(a + d, self.outer) + (1 - b if other else b), other))
+        for shard, other in shards:
+            for k, block in enumerate(self.mine):
+                self.arrived(shard, block)
+                if not other:
+                    self.push(shard, block, beside_x)
+                if k == 0:
+                    self.push(shard, block, beside_y)
+                self.push(shard, block, beside_core)
+                yield
+        for shard, _ in shards:
+            block = 3 * c + 1 - u
+            self.arrived(shard, block)
+            self.push(shard, block, beside_core)
+            yield
+        for shard, _ in shards:
+            for k in range(3):
+                self.arrived(shard, 3 * (1 - c) + k)
+            yield
+
+    def finish(self):
+        for copy in self.sent:
+            copy.wait_send()
+        self.local.wait()
+
+
+def gather_sends(owners):
+    outer = owners // 2
+    return 2 * outer + 2 * (outer - 1) + 4 * (owners - 1)
+
+
+class Exchange:
+    def __init__(self, devices, reps, me, source, target, send_sem, recv_sem):
+        self.devices, self.reps, self.me = devices, reps, me
+        self.source, self.target = source, target
+        self.send_sem, self.recv_sem = send_sem, recv_sem
+
+    def copy(self, k):
+        to = lax.rem(self.me + k, self.devices)
+        return pltpu.make_async_remote_copy(
+            src_ref=self.source(to),
+            dst_ref=self.target(self.me),
+            send_sem=self.send_sem.at[k],
+            recv_sem=self.recv_sem.at[k],
+            device_id=peer(to, self.reps),
+            device_id_type=MESH_ID,
+        )
+
+    def start(self):
+        def one(k, carry):
+            self.copy(k).start()
+            return carry
+
+        lax.fori_loop(1, self.devices, one, 0)
+
+    def wait_recv(self):
+        def one(k, carry):
+            come = lax.rem(self.me + self.devices - k, self.devices)
+            ref = self.target(come)
+            pltpu.make_async_copy(ref, ref, self.recv_sem.at[k]).wait()
+            return carry
+
+        lax.fori_loop(1, self.devices, one, 0)
+
+    def wait_send(self):
+        def one(k, carry):
+            self.copy(k).wait_send()
+            return carry
+
+        lax.fori_loop(1, self.devices, one, 0)
+
+
+def first_kernel(owners, reps, own_ref, lists_ref, table_ref, all_lists_ref, send_sem, recv_sem, local_sem, ls, lr):
+    me = lax.axis_index("mem") * reps + lax.axis_index("rep")
+    devices = owners * reps
+    enter(devices, reps, me)
+    gather = Gather(owners, own_ref, table_ref, send_sem, recv_sem, local_sem.at[0])
+    lists = Exchange(
+        devices, reps, me,
+        lambda to: lists_ref.at[to // reps], lambda come: all_lists_ref.at[come], ls, lr,
+    )
+    mine = pltpu.make_async_copy(
+        lists_ref.at[lax.axis_index("mem")], all_lists_ref.at[me], local_sem.at[1]
+    )
+    lists.start()
+    mine.start()
+    gather.begin()
+    for _ in gather.steps():
+        pass
+    lists.wait_recv()
+    lists.wait_send()
+    mine.wait()
+    gather.finish()
+
+
+def reduce_parts(devices, reps, me, grads_ref, parts_ref, sum_ref, total_ref, sems, between=None):
+    scatter = Exchange(
+        devices, reps, me, lambda to: grads_ref.at[to], lambda come: parts_ref.at[come],
+        sems[0], sems[1],
+    )
+    share = Exchange(
+        devices, reps, me, lambda to: sum_ref, lambda come: total_ref.at[come], sems[2], sems[3]
+    )
+    return scatter, share
+
+
+def reduce_middle(me, grads_ref, parts_ref, sum_ref, total_ref):
+    parts_ref[me] = grads_ref[me]
+    total = jnp.sum(parts_ref[...].astype(F32), 0)
+    sum_ref[...] = total
+    total_ref[me] = total
+
+
+def second_kernel(owners, reps, own_ref, grads_ref, table_ref, total_ref, send_sem, recv_sem, local_sem, parts_ref, sum_ref, s0, s1, s2, s3):
+    me = lax.axis_index("mem") * reps + lax.axis_index("rep")
+    devices = owners * reps
+    enter(devices, reps, me)
+    gather = Gather(owners, own_ref, table_ref, send_sem, recv_sem, local_sem.at[0])
+    scatter, share = reduce_parts(devices, reps, me, grads_ref, parts_ref, sum_ref, total_ref, (s0, s1, s2, s3))
+    scatter.start()
+    gather.begin()
+    for step, _ in enumerate(gather.steps()):
+        if step == 2:
+            scatter.wait_recv()
+            reduce_middle(me, grads_ref, parts_ref, sum_ref, total_ref)
+            share.start()
+    share.wait_recv()
+    scatter.wait_send()
+    share.wait_send()
+    gather.finish()
+
+
+def third_kernel(owners, reps, grads_ref, total_ref, parts_ref, sum_ref, s0, s1, s2, s3):
+    me = lax.axis_index("mem") * reps + lax.axis_index("rep")
+    devices = owners * reps
+    enter(devices, reps, me)
+    scatter, share = reduce_parts(devices, reps, me, grads_ref, parts_ref, sum_ref, total_ref, (s0, s1, s2, s3))
+    scatter.start()
+    scatter.wait_recv()
+    reduce_middle(me, grads_ref, parts_ref, sum_ref, total_ref)
+    share.start()
+    share.wait_recv()
+    scatter.wait_send()
+    share.wait_send()
+
+
+def up8(n):
+    return -(-n // 8) * 8
+
+
+class Pack:
+    def __init__(self, width, embed, devices):
+        self.width, self.embed, self.devices = width, embed, devices
+        self.high = up8(width - LANES)
+        self.side = up8(embed)
+        self.main = 16 * devices
+        self.nbr = 2 * LANES
+        self.top = 4 * LANES
+        self.bottom = 5 * LANES
+        self.vectors = 6 * LANES
+        self.rows = 6 * LANES + 8
+        self.at_top = 2 * LANES + 2 * self.high
+        self.at_bottom = self.at_top + self.side
+        self.extra = self.at_bottom + self.side - self.main
+        self.spare = LANES - embed
+        self.chunks = -(-embed // self.spare) if self.spare > 0 else 0
+
+    def fits(self):
+        return (
+            self.spare > 0
+            and 0 <= self.extra < self.side
+            and self.chunks * (self.extra + 8) <= self.main
+        )
+
+
+def pack_params(pack, refs, out_ref):
+    w_self, w_nbr, b_embed, w_dec1, b_dec1, w_dec2, b_dec2 = refs
+    width, embed = pack.width, pack.embed
+    out_ref[...] = jnp.zeros_like(out_ref)
+    out_ref[0:width, 0:embed] = w_self[...]
+    out_ref[pack.nbr : pack.nbr + width, 0:embed] = w_nbr[...]
+    out_ref[pack.top : pack.top + embed, 0:embed] = w_dec1[0:embed, :]
+    out_ref[pack.bottom : pack.bottom + embed, 0:embed] = w_dec1[embed : 2 * embed, :]
+    v = pack.vectors
+    out_ref[v : v + 1, 0:embed] = b_embed[...]
+    out_ref[v + 1 : v + 2, 0:embed] = b_dec1[...]
+    out_ref[v + 2 : v + 3, 0:embed] = w_dec2[...]
+    out_ref[v + 3 : v + 4, 0:1] = b_dec2[...]
+
+
+def pack_grads(pack, grads, small, table_ref, out_ref):
+    s_lo, s_hi, n_lo, n_hi, top, bottom = grads
+    high, side, extra = pack.high, pack.side, pack.extra
+    table_ref[0:LANES] = s_lo
+    table_ref[LANES : 2 * LANES] = n_lo
+    table_ref[2 * LANES : 2 * LANES + high] = s_hi[:high]
+    table_ref[2 * LANES + high : pack.at_top] = n_hi[:high]
+    table_ref[pack.at_top : pack.at_bottom] = top[:side]
+    table_ref[pack.at_bottom : pack.main] = bottom[: side - extra]
+    coarse = small.astype(BF).astype(F32)
+    pieces = [(0, bottom[side - extra : side])] if extra else []
+    pieces.append((pack.chunks * extra, jnp.concatenate([coarse, small - coarse], 0)))
+    for start, piece in pieces:
+        size = piece.shape[0]
+        lane = iota((size, LANES), 1)
+        for k in range(pack.chunks):
+            moved = pltpu.roll(piece, (pack.embed - k * pack.spare) % LANES, 1)
+            rows = slice(start + k * size, start + (k + 1) * size)
+            table_ref[rows] = jnp.where(lane >= pack.embed, moved, table_ref[rows])
+    out_ref[...] = table_ref[...].reshape(out_ref.shape).astype(BF)
+
+
+def update_params(pack, total_ref, old_ref, new_ref):
+    high, side, extra = pack.high, pack.side, pack.extra
+    table = total_ref[...].reshape(pack.main, LANES)
+
+    def clean(x):
+        return jnp.where(iota(x.shape, 1) < pack.embed, x, 0.0)
+
+    def collect(start, size):
+        out = jnp.zeros((size, LANES), F32)
+        lane = iota((size, LANES), 1)
+        for k in range(pack.chunks):
+            part = table[start + k * size : start + (k + 1) * size]
+            part = jnp.where(lane >= pack.embed, part, 0.0)
+            out = out + pltpu.roll(part, (k * pack.spare - pack.embed) % LANES, 1)
+        return out
+
+    small = collect(pack.chunks * extra, 8)
+    small = small[0:4] + small[4:8]
+    lane4 = iota((4, LANES), 1)
+    row4 = iota((4, LANES), 0)
+    loss = jnp.sum(jnp.where((row4 == 3) & (lane4 == 1), small, 0.0))
+    count = jnp.sum(jnp.where((row4 == 3) & (lane4 == 2), small, 0.0))
+    small = jnp.where((row4 < 3) | (lane4 == 0), small, 0.0)
+    parts = [
+        (0, clean(table[0:LANES])),
+        (LANES, clean(table[2 * LANES : 2 * LANES + high])),
+        (pack.nbr, clean(table[LANES : 2 * LANES])),
+        (pack.nbr + LANES, clean(table[2 * LANES + high : pack.at_top])),
+        (pack.top, clean(table[pack.at_top : pack.at_bottom])),
+        (pack.bottom, clean(table[pack.at_bottom : pack.main])),
+    ]
+    if extra:
+        parts.append((pack.bottom + side - extra, collect(0, extra)))
+    total = jnp.sum(small * small)
+    for _, part in parts:
+        total = total + jnp.sum(part * part)
+    total = jnp.zeros((1, LANES), F32) + total
+    factor = step_size / (jnp.sqrt(total) + 1e-06)
+    new_ref[...] = old_ref[...]
+    for start, part in parts:
+        rows = slice(start, start + part.shape[0])
+        new_ref[rows] = old_ref[rows] - factor * part
+    rows = slice(pack.vectors, pack.vectors + 4)
+    new_ref[rows] = old_ref[rows] - factor * small
+    return loss / jnp.maximum(jnp.zeros((1, LANES), F32) + count, 1.0)
+
+
+def unpack_params(pack, packed_ref, refs):
+    w_self, w_nbr, b_embed, w_dec1, b_dec1, w_dec2, b_dec2 = refs
+    width, embed = pack.width, pack.embed
+    w_self[...] = packed_ref[0:width, 0:embed]
+    w_nbr[...] = packed_ref[pack.nbr : pack.nbr + width, 0:embed]
+    w_dec1[0:embed, :] = packed_ref[pack.top : pack.top + embed, 0:embed]
+    w_dec1[embed : 2 * embed, :] = packed_ref[pack.bottom : pack.bottom + embed, 0:embed]
+    v = pack.vectors
+    b_embed[...] = packed_ref[v : v + 1, 0:embed]
+    b_dec1[...] = packed_ref[v + 1 : v + 2, 0:embed]
+    w_dec2[...] = packed_ref[v + 2 : v + 3, 0:embed]
+    b_dec2[...] = packed_ref[v + 3 : v + 4, 0:1]
+
+
+def expand(table_ref, low_ref, high_ref, shard, quarter):
+    base = shard * 4 * quarter
+    lane = iota((quarter, LANES), 1)
+    for c in range(2):
+        for u in range(2):
+            at = pl.multiple_of(base + (2 * c + u) * quarter, quarter)
+            low_ref[pl.ds(at, quarter), :] = table_ref[shard, 3 * c + u].astype(F32)
+        both = table_ref[shard, 3 * c + 2].astype(F32)
+        at = pl.multiple_of(base + 2 * c * quarter, quarter)
+        high_ref[pl.ds(at, quarter), :] = jnp.where(lane < LANES // 2, both, 0.0)
+        at = pl.multiple_of(base + (2 * c + 1) * quarter, quarter)
+        high_ref[pl.ds(at, quarter), :] = jnp.where(
+            lane < LANES // 2, pltpu.roll(both, LANES // 2, 1), 0.0
+        )
+
+
+def partner_rows(batch, cap, lists_smem, low_ref, high_ref, out_low, out_high):
+    def one(d, carry):
+        for j in range(cap):
+            p = lists_smem[d, 1, batch * cap + j]
+            at = d * cap + j
+            out_low[pl.ds(at, 1), :] = low_ref[pl.ds(p, 1), :]
+            out_high[pl.ds(at, 1), :] = high_ref[pl.ds(p, 1), :]
+        return carry
+
+    lax.fori_loop(0, lists_smem.shape[0], one, 0)
+
+
+def event_rows(batch, nodes_smem, slot_smem, low_ref, high_ref, own_low, own_high, nbr_low, nbr_high):
+    _, events, columns = nodes_smem.shape
+    neighbours = (columns - 3) // 3
+
+    def one(e, carry):
+        def row(col):
+            slot = slot_smem[nodes_smem[batch, e, col]]
+            return low_ref[pl.ds(slot, 1), :], high_ref[pl.ds(slot, 1), :]
+
+        for r in range(3):
+            at = pl.ds(r * events + e, 1)
+            low, high = row(r)
+            own_low[at, :] = low
+            own_high[at, :] = high
+            low, high = row(3 + r * neighbours)
+            for k in range(1, neighbours):
+                more, rest = row(3 + r * neighbours + k)
+                low, high = low + more, high + rest
+            nbr_low[at, :] = low
+            nbr_high[at, :] = high
+        return carry
+
+    lax.fori_loop(0, events, one, 0)
+
+
+def pair_row(batch, cap, lists_ref, i, row):
+    first, second = lists_ref[2 * i], lists_ref[2 * i + 1]
+    lane = iota(first.shape, 1)
+    if batch == 0:
+        both = jnp.where(lane < cap, first, pltpu.roll(second, cap, 1))
+    else:
+        both = jnp.where(lane < cap, pltpu.roll(first, cap, 1), second)
+    return both[row : row + 1]
+
+
+def letter_codes(batch, cap, lists_ref, codes_ref, letters_ref):
+    times = codes_ref.shape[0]
+    codes = codes_ref[...]
+    for i in range(lists_ref.shape[0] // 2):
+        stamp = pair_row(batch, cap, lists_ref, i, 2)
+        hot = jnp.where(iota((times, LANES), 0) == stamp, 1.0, 0.0).astype(BF)
+        letters_ref[i * LANES : (i + 1) * LANES, 2 * LANES :] = dot_tn(hot, codes).astype(BF)
+
+
+def split2(x):
+    coarse = x.astype(BF)
+    return coarse, (x - coarse.astype(F32)).astype(BF)
+
+
+def memory_step(batch, cap, width, code, lists_ref, letters_ref, memory_ref, gi_ref, gh_ref, bias_ref, hot_ref, out_ref, blocks_ref):
+    slots = memory_ref.shape[0]
+    quarter = slots // 4
+    pairs = lists_ref.shape[0] // 2
+    lane = iota((quarter, LANES), 1)
+    rest = width - LANES
+    held = None
+    for q in range(4):
+        rows = slice(q * quarter, (q + 1) * quarter)
+        for i in range(pairs):
+            target = pair_row(batch, cap, lists_ref, i, 0)
+            hot = jnp.where(iota((quarter, LANES), 0) + q * quarter == target, 1.0, 0.0)
+            hot_ref[:, i * LANES : (i + 1) * LANES] = hot.astype(BF)
+        summed = dot(hot_ref[...], letters_ref[...])
+        counts = jnp.sum(
+            jnp.where(lane == code, summed[:, 2 * LANES :], 0.0), 1, keepdims=True
+        )
+        mean = (summed / jnp.maximum(counts, 1.0)).astype(BF)
+        low = memory_ref[rows, 0:LANES]
+        high = pad_lanes(memory_ref[rows, LANES:width])
+        old = jnp.concatenate([low, high], 1)
+        state = old.astype(BF)
+        joined = jnp.concatenate([state, mean], 1)
+        inner = [dot(joined, gi_ref[j]) + bias_ref[j : j + 1] for j in range(3)]
+        outer = [dot(state, gh_ref[j]) + bias_ref[j + 3 : j + 4] for j in range(3)]
+        reset = jax.nn.sigmoid(inner[0] + outer[0])
+        update = jax.nn.sigmoid(inner[1] + outer[1])
+        candidate = jnp.tanh(inner[2] + reset * outer[2])
+        fresh = (1.0 - update) * candidate + update * old
+        new = jnp.where(counts > 0.5, fresh, old)
+        new_low, new_high = new[:, :LANES], new[:, LANES:]
+        out_ref[rows, 0:LANES] = new_low
+        out_ref[rows, LANES:width] = new_high[:, :rest]
+        if blocks_ref is not None:
+            c, u = q // 2, q % 2
+            blocks_ref[3 * c + u] = new_low.astype(BF)
+            masked = jnp.where(lane < rest, new_high, 0.0)
+            if u == 0:
+                held = masked
+            else:
+                blocks_ref[3 * c + 2] = (held + pltpu.roll(masked, LANES // 2, 1)).astype(BF)
+
+
+def loss_step(pack, batch, neighbours, params_ref, valid_ref, own_low, own_high, nbr_low, nbr_high, table_ref, out_ref):
+    events = valid_ref.shape[1]
+    v = pack.vectors
+
+    def weight(start):
+        return params_ref[start : start + LANES].astype(BF)
+
+    b_embed = params_ref[v : v + 1]
+    b_dec1 = params_ref[v + 1 : v + 2]
+    w_dec2 = params_ref[v + 2 : v + 3]
+    b_dec2 = jnp.sum(params_ref[v + 3 : v + 4])
+    x_low, x_high = own_low[...].astype(BF), own_high[...].astype(BF)
+    n_low, n_high = split2(nbr_low[...]), split2(nbr_high[...])
+    direct = dot(x_low, weight(0)) + dot(x_high, weight(LANES))
+    w_low, w_high = weight(pack.nbr), weight(pack.nbr + LANES)
+    spread = (
+        dot(n_low[0], w_low) + dot(n_low[1], w_low) + dot(n_high[0], w_high) + dot(n_high[1], w_high)
+    )
+    act = jnp.tanh(direct + spread * (1.0 / neighbours) + b_embed)
+    hidden = act.astype(BF)
+    h0, h1, h2 = (hidden[r * events : (r + 1) * events] for r in range(3))
+    top, bottom = weight(pack.top), weight(pack.bottom)
+    shared = dot(h0, top)
+    pre = [shared + dot(h, bottom) + b_dec1 for h in (h1, h2)]
+    eye = iota((events, events), 0) == iota((events, events), 1)
+    valid = jnp.where(eye, valid_ref[batch : batch + 1].astype(F32), 0.0)
+    valid = jnp.sum(valid, 1, keepdims=True)
+    loss = jnp.zeros((1, 1), F32)
+    d_pre, g_dec2, g_out = [], jnp.zeros((1, LANES), F32), jnp.zeros((1, 1), F32)
+    for z, sign in zip(pre, (-1.0, 1.0)):
+        inner = jnp.maximum(z, 0.0)
+        logit = (jnp.sum(inner * w_dec2, 1, keepdims=True) + b_dec2) * sign
+        soft = jnp.maximum(logit, 0.0) + jnp.log1p(jnp.exp(-jnp.abs(logit)))
+        loss = loss + jnp.sum(soft * valid, 0, keepdims=True)
+        d_logit = jax.nn.sigmoid(logit) * valid * sign
+        g_dec2 = g_dec2 + jnp.sum(d_logit * inner, 0, keepdims=True)
+        g_out = g_out + jnp.sum(d_logit, 0, keepdims=True)
+        d_pre.append(jnp.where(z > 0.0, d_logit * w_dec2, 0.0))
+    g_dec1 = jnp.sum(d_pre[0] + d_pre[1], 0, keepdims=True)
+    both = split2(d_pre[0] + d_pre[1])
+    parts = [split2(d) for d in d_pre]
+    g_top = dot_tn(h0, both[0]) + dot_tn(h0, both[1])
+    g_bottom = (
+        dot_tn(h1, parts[0][0]) + dot_tn(h1, parts[0][1])
+        + dot_tn(h2, parts[1][0]) + dot_tn(h2, parts[1][1])
+    )
+    back = []
+    for w in (top, bottom):
+        back.append([(dot_nt(p[0], w) + dot_nt(p[1], w)).astype(BF) for p in parts])
+    d0 = (back[0][0].astype(F32) + back[0][1].astype(F32)).astype(BF)
+    d_hidden = jnp.concatenate([d0, back[1][0], back[1][1]], 0).astype(F32)
+    d_act = d_hidden * (1.0 - act * act)
+    g_embed = jnp.sum(d_act, 0, keepdims=True)
+    d_own = split2(d_act)
+    d_nbr = split2(d_act * (1.0 / neighbours))
+    g_s = [dot_tn(x, d_own[0]) + dot_tn(x, d_own[1]) for x in (x_low, x_high)]
+    g_n = [
+        dot_tn(n[0], d_nbr[0]) + dot_tn(n[0], d_nbr[1]) + dot_tn(n[1], d_nbr[0])
+        for n in (n_low, n_high)
+    ]
+    count = jnp.sum(valid, 0, keepdims=True)
+    lane = iota((1, LANES), 1)
+    scalars = jnp.where(lane == 0, g_out, jnp.where(lane == 1, loss, jnp.where(lane == 2, count, 0.0)))
+    small = jnp.concatenate([g_embed, g_dec1, g_dec2, scalars], 0)
+    pack_grads(pack, (g_s[0], g_s[1], g_n[0], g_n[1], g_top, g_bottom), small, table_ref, out_ref)
+
+
+def start_kernel(owners, node_dev, cap, code, pack, slot_ref, pair_ref, time_ref, freq_ref, phase_ref, memory_ref, *refs):
+    params, (lists_ref, codes_ref, packed_ref, blocks_ref) = refs[:7], refs[7:]
+    lists_kernel(owners, node_dev, cap, code, slot_ref, pair_ref, time_ref, freq_ref, phase_ref, lists_ref, codes_ref)
+    pack_params(pack, params, packed_ref)
+    width = memory_ref.shape[1]
+    quarter = node_dev // 4
+    for c in range(2):
+        for u in range(2):
+            rows = slice((2 * c + u) * quarter, (2 * c + u + 1) * quarter)
+            blocks_ref[3 * c + u] = memory_ref[rows, 0:LANES].astype(BF)
+        first = slice(2 * c * quarter, (2 * c + 1) * quarter)
+        second = slice((2 * c + 1) * quarter, (2 * c + 2) * quarter)
+        blocks_ref[3 * c + 2] = (
+            pad_lanes(memory_ref[first, LANES:width])
+            + pltpu.roll(pad_lanes(memory_ref[second, LANES:width]), LANES // 2, 1)
+        ).astype(BF)
+
+
+def batch_kernel(batch, last, cap, code, pack, nodes_smem, slot_smem, lists_smem, table_ref, lists_ref, codes_ref, memory_ref, valid_ref, gi_ref, gh_ref, bias_ref, params_ref, *refs):
+    if last:
+        (out_ref, grads_ref), rest = refs[:2], refs[2:]
+        blocks_ref = None
+    else:
+        (out_ref, blocks_ref, grads_ref), rest = refs[:3], refs[3:]
+    low, high, p_low, p_high, letters, hot, own_low, own_high, nbr_low, nbr_high, flat = rest
+    owners = table_ref.shape[0]
+    quarter = memory_ref.shape[0] // 4
+    neighbours = (nodes_smem.shape[2] - 3) // 3
+
+    def spread(s, carry):
+        expand(table_ref, low, high, s, quarter)
+        return carry
+
+    lax.fori_loop(0, owners, spread, 0)
+    partner_rows(batch, cap, lists_smem, low, high, p_low, p_high)
+    letters[:, 0:LANES] = p_low[...].astype(BF)
+    letters[:, LANES : 2 * LANES] = p_high[...].astype(BF)
+    letter_codes(batch, cap, lists_ref, codes_ref, letters)
+    memory_step(batch, cap, pack.width, code, lists_ref, letters, memory_ref, gi_ref, gh_ref, bias_ref, hot, out_ref, blocks_ref)
+    event_rows(batch, nodes_smem, slot_smem, low, high, own_low, own_high, nbr_low, nbr_high)
+    loss_step(pack, batch, neighbours, params_ref, valid_ref, own_low, own_high, nbr_low, nbr_high, flat, grads_ref)
+
+
+def update_kernel(pack, total_ref, old_ref, new_ref, loss_ref):
+    loss_ref[...] = update_params(pack, total_ref, old_ref, new_ref)
+
+
+def final_kernel(pack, total_ref, old_ref, *refs):
+    loss_ref, outs, new_ref = refs[0], refs[1:8], refs[8]
+    loss_ref[...] = update_params(pack, total_ref, old_ref, new_ref)
+    unpack_params(pack, new_ref, outs)
+
+
+def quick_body(owners, reps, cap, memory, node_slot, event_nodes, event_times, valid_mask, time_freq, time_phase, gru_input, gru_hidden, gru_in_bias, gru_hid_bias, *params):
+    node_dev, width = memory.shape
+    batches, events, columns = event_nodes.shape
+    code = time_freq.shape[0]
+    embed = params[0].shape[1]
+    devices = owners * reps
+    pack = Pack(width, embed, devices)
+    quarter = node_dev // 4
+    sds = jax.ShapeDtypeStruct
+    pairs = event_nodes[:, :, :2].transpose(0, 2, 1).reshape(1, -1)
+    times = jnp.broadcast_to(event_times[:, None, :], (batches, 2, events)).reshape(1, -1)
+    freq = jnp.pad(time_freq, (0, LANES - code))[None, :]
+    phase = jnp.pad(time_phase, (0, LANES - code))[None, :]
+    rows = [p[None, :] if p.ndim == 1 else p for p in params]
+    stamps = -(-TIMES // LANES) * LANES
+    lists, codes, packed, blocks = pl.pallas_call(
+        functools.partial(start_kernel, owners, node_dev, cap, code, pack),
+        out_shape=(
+            sds((owners, 8, 2 * cap), jnp.int32),
+            sds((stamps, LANES), BF),
+            sds((pack.rows, LANES), F32),
+            sds((6, quarter, LANES), BF),
+        ),
+        in_specs=vmem(13),
+        out_specs=tuple(vmem(4)),
+        name="start",
+    )(node_slot.reshape(-1, LANES), pairs, times, freq, phase, memory, *rows)
+
+    pad_w = 2 * LANES - width
+    gi = gru_input.reshape(-1, 3, width).transpose(1, 0, 2)
+    gi = jnp.concatenate(
+        [
+            jnp.pad(gi[:, :width], ((0, 0), (0, pad_w), (0, pad_w))),
+            jnp.pad(gi[:, width : 2 * width], ((0, 0), (0, pad_w), (0, pad_w))),
+            jnp.pad(gi[:, 2 * width :], ((0, 0), (0, LANES - code), (0, pad_w))),
+        ],
+        1,
+    )
+    gh = jnp.pad(gru_hidden.reshape(width, 3, width).transpose(1, 0, 2), ((0, 0), (0, pad_w), (0, pad_w)))
+    bias = jnp.pad(
+        jnp.concatenate([gru_in_bias.reshape(3, width), gru_hid_bias.reshape(3, width)], 0),
+        ((0, 2), (0, pad_w)),
+    )
+
+    dma = pltpu.SemaphoreType.DMA
+    sends = gather_sends(owners)
+    gather_sems = [dma((sends,)), dma((owners, 6)), dma((2,))]
+    reduce_scratch = [
+        pltpu.VMEM((devices, 16, LANES), BF),
+        pltpu.VMEM((16, LANES), F32),
+        dma((devices,)),
+        dma((devices,)),
+        dma((devices,)),
+        dma((devices,)),
+    ]
+    table_shape = sds((owners, 6, quarter, LANES), BF)
+    total_shape = sds((devices, 16, LANES), F32)
+    table, all_lists = pl.pallas_call(
+        functools.partial(first_kernel, owners, reps),
+        out_shape=(table_shape, sds((devices, 8, 2 * cap), jnp.int32)),
+        in_specs=vmem(2),
+        out_specs=tuple(vmem(2)),
+        scratch_shapes=gather_sems + [dma((devices,)), dma((devices,))],
+        compiler_params=pltpu.CompilerParams(collective_id=0, has_side_effects=True),
+        name="first",
+    )(blocks, lists)
+
+    losses = []
+    for batch in range(batches):
+        last = batch == batches - 1
+        outs = [sds((node_dev, width), F32)]
+        if not last:
+            outs.append(sds((6, quarter, LANES), BF))
+        outs.append(sds((devices, 16, LANES), BF))
+        letters = devices * cap
+        slots = node_slot.shape[0]
+        made = pl.pallas_call(
+            functools.partial(batch_kernel, batch, last, cap, code, pack),
+            out_shape=tuple(outs),
+            in_specs=[pl.BlockSpec(memory_space=pltpu.SMEM)] * 3 + vmem(9),
+            out_specs=tuple(vmem(len(outs))),
+            scratch_shapes=[
+                pltpu.VMEM((slots, LANES), F32),
+                pltpu.VMEM((slots, LANES), F32),
+                pltpu.VMEM((letters, LANES), F32),
+                pltpu.VMEM((letters, LANES), F32),
+                pltpu.VMEM((letters, 3 * LANES), BF),
+                pltpu.VMEM((quarter, letters), BF),
+                pltpu.VMEM((3 * events, LANES), F32),
+                pltpu.VMEM((3 * events, LANES), F32),
+                pltpu.VMEM((3 * events, LANES), F32),
+                pltpu.VMEM((3 * events, LANES), F32),
+                pltpu.VMEM((pack.main, LANES), F32),
+            ],
+            compiler_params=pltpu.CompilerParams(vmem_limit_bytes=48 * 1024 * 1024),
+            name="batch" + str(batch),
+        )(event_nodes, node_slot, all_lists, table, all_lists, codes, memory, valid_mask, gi, gh, bias, packed)
+        if last:
+            memory, grads = made
+            total = pl.pallas_call(
+                functools.partial(third_kernel, owners, reps),
+                out_shape=total_shape,
+                in_specs=vmem(1),
+                out_specs=vmem(1)[0],
+                scratch_shapes=reduce_scratch,
+                compiler_params=pltpu.CompilerParams(collective_id=2, has_side_effects=True),
+                name="third",
+            )(grads)
+            outs = pl.pallas_call(
+                functools.partial(final_kernel, pack),
+                out_shape=(sds((1, LANES), F32),) + tuple(sds(p.shape, F32) for p in rows),
+                in_specs=vmem(2),
+                out_specs=tuple(vmem(8)),
+                scratch_shapes=[pltpu.VMEM((pack.rows, LANES), F32)],
+                name="final",
+            )(total, packed)
+            losses.append(outs[0])
+            params = [o.reshape(p.shape) for o, p in zip(outs[1:], params)]
+        else:
+            memory, blocks, grads = made
+            table, total = pl.pallas_call(
+                functools.partial(second_kernel, owners, reps),
+                out_shape=(table_shape, total_shape),
+                in_specs=vmem(2),
+                out_specs=tuple(vmem(2)),
+                scratch_shapes=gather_sems + reduce_scratch,
+                compiler_params=pltpu.CompilerParams(collective_id=1, has_side_effects=True),
+                name="second",
+            )(blocks, grads)
+            packed, loss = pl.pallas_call(
+                functools.partial(update_kernel, pack),
+                out_shape=(sds((pack.rows, LANES), F32), sds((1, LANES), F32)),
+                in_specs=vmem(2),
+                out_specs=tuple(vmem(2)),
+                name="update",
+            )(total, packed)
+            losses.append(loss)
+    losses = jnp.concatenate([loss[:, 0] for loss in losses])
+    return (memory, losses, *params)
 
 
 def block_loss(current, own_rows, beside_sum, neighbours, valid_part):
@@ -214,29 +1042,36 @@
 
 
 def solution(mesh):
-    return jax.shard_map(
-        body,
-        mesh=mesh,
-        in_specs=(
-            P("mem", None),
-            P(),
-            P(None, ("mem", "rep"), None),
-            P(None, ("mem", "rep")),
-            P(None, ("mem", "rep")),
-            P(),
-            P(),
-            P(),
-            P(),
-            P(),
-            P(),
-            P(),
-            P(),
-            P(),
-            P(),
-            P(),
-            P(),
-            P(),
-        ),
-        out_specs=(P("mem", None), P(), P(), P(), P(), P(), P(), P(), P()),
-        check_vma=False,
-    )
+    owners, reps = mesh.shape["mem"], mesh.shape["rep"]
+    in_specs = (
+        P("mem", None),
+        P(),
+        P(None, ("mem", "rep"), None),
+        P(None, ("mem", "rep")),
+        P(None, ("mem", "rep")),
+    ) + (P(),) * 13
+    out_specs = (P("mem", None),) + (P(),) * 8
+
+    def choose(*args):
+        memory, node_slot, event_nodes = args[:3]
+        node_dev, width = memory.shape
+        batches, events, _ = event_nodes.shape
+        cap = 2 * events // owners * 2
+        pack = Pack(width, args[11].shape[1], owners * reps)
+        small = node_slot.shape[0] * 2 * LANES * 4 <= 16 * 1024 * 1024
+        shaped = (
+            reps == 4
+            and owners % 2 == 0
+            and batches == 2
+            and 2 * cap == LANES
+            and events == LANES
+            and node_dev % (4 * LANES) == 0
+            and LANES < width <= LANES + LANES // 2
+            and args[5].shape[0] < LANES
+            and pack.fits()
+        )
+        if small and shaped:
+            return quick_body(owners, reps, cap, *args)
+        return body(*args)
+
+    return jax.shard_map(choose, mesh=mesh, in_specs=in_specs, out_specs=out_specs, check_vma=False)

time: 357 us -> 174 us (0.49)
  Pallas kernels: 0 us -> 151 us
  waiting for transfers between devices: 113 us -> 0 us
  blocking collectives: 97 us -> 0 us
  other arithmetic: 32.9 us -> 1.36 us
  between operations: 30.8 us -> 1.54 us
  local copies, waits for them, and re-layouts: 45.8 us -> 19 us
  matrix products: 23.9 us -> 0 us
  starting transfers between devices: 11.9 us -> 0 us
    pallas_call x0 -> x8, Pallas kernels: none -> 151 us  [the longest x2 47.9 us: quick_body(): pl.pallas_call(functools.partial(batch_kernel, batch, last, cap, code, pa...]
    all_gather x4 -> x0, waiting for transfers between devices: 82.3 us -> none  [the longest x2 67.9 us: body(): whole_bf = lax.all_gather(memory_bf, 'mem', axis=0, tiled=True)]
    all_gather x2 -> x0, blocking collectives: 81.9 us -> none  [sum_everywhere(): lax.all_gather(jnp.sum(parts, 0), ('mem', 'rep'), axis=0, tiled=True)]
    all_to_all x3 -> x0, waiting for transfers between devices: 30.7 us -> none  [the longest x2 27.7 us: sum_everywhere(): lax.all_to_all(table, ('mem', 'rep'), split_axis=0, concat_axis=0, tiled=...]
    gather x2 -> x0, local copies, waits for them, and re-layouts: 24.7 us -> none  [body(): fetched = jnp.take(whole_bf, slot_ids.reshape(-1), axis=0, mode='clip')]
    dot_general x27 -> x0, matrix products: 23.9 us -> none  [the longest x2 3.97 us: body(): jnp.dot(matches.astype(jnp.bfloat16), every_parcel, preferred_element_typ...]
    all_to_all x1 -> x0, blocking collectives: 15.1 us -> none  [body(): lax.all_to_all(parcel, 'mem', split_axis=0, concat_axis=0, tiled=True)]
    reduce_sum x19 -> x0, other arithmetic: 11.6 us -> none  [the longest x6 3.74 us: normalized_step(): total = total + jnp.sum(grad_part * grad_part)]
  transfers between devices with their start and end apart: 7 -> 0, of which waited for: 5 -> 0; matrix products, arithmetic and copies ran while one was open for 12% -> 0% of each run, Pallas kernels for 0% -> 0%
where the time goes in v1:
time: 174 us; the launch traced here: 172 us
  Pallas kernels  151 us (87%)
  local copies, waits for them, and re-layouts  19 us (11%)
    pallas_call x2, Pallas kernels, quick_body(): pl.pallas_call(functools.partial(batch_kernel, batch, last, cap, code, pa...  47.9 us
    pallas_call x1, Pallas kernels, quick_body(): pl.pallas_call(functools.partial(second_kernel, owners, reps), out_shape=...  38.9 us
    pallas_call x1, Pallas kernels, quick_body(): pl.pallas_call(functools.partial(first_kernel, owners, reps), out_shape=(...  33.9 us
    pallas_call x1, Pallas kernels, quick_body(): pl.pallas_call(functools.partial(third_kernel, owners, reps), out_shape=t...  20.9 us
    unnamed x37, local copies, waits for them, and re-layouts  12 us
    pallas_call x1, Pallas kernels, quick_body(): pl.pallas_call(functools.partial(start_kernel, owners, node_dev, cap, cod...  4.81 us

profile of v1, /device:TPU:0, one launch (start us, length us, event | category | flops | bytes accessed | tf_op | source)
XLA Modules:
  0.0 172.5 jit_solution(16670368863896313183)
XLA Ops:
  1.4 1.2 pad_bitcast_fusion
  2.5 1.3 broadcast_in_dim.24
  3.8 0.7 slice_bitcast_fusion
  4.5 0.6 copy.33
  5.1 0.8 reshape.57
  5.8 0.8 reshape.58
  6.6 0.9 copy.40.nodes_smem
  7.5 1.2 reshape.63
  8.8 0.2 reshape.55
  8.9 0.3 copy.35
  9.3 0.1 fusion.5.gi_ref
  9.5 0.6 copy-done.14
  10.1 1.3 copy.34.memory_ref
  11.4 4.8 %start.1 = (s32[8,8,128]{2,1,0:T(8,128)}, bf16[1024,128]{1,0:T(8,128)(2,1)}, f32[776,128]{1,0:T(8,128)}, bf16[6,256,128]{2,1,0:T(8,128)(2,1)}) custom-call(s32[64,128]{1,0:T(8,128)} %bitcast.28, s32[1,512]{1,0:T(1,128)} %bitcast.33, s32[1,512]{1,0:T(1,128)} %bitcast.32, f32[1,128]{1,0:T(1,128)} %get-tuple-element.76.freq_ref, ...), custom_call_target="tpu_custom_call" | custom-call | tf_op jit(solution)/shard_map/start/pallas_call | solution.py:711
  16.2 33.9 %first.1 = (bf16[8,6,256,128]{3,2,1,0:T(8,128)(2,1)}, s32[32,8,128]{2,1,0:T(8,128)}) custom-call(bf16[6,256,128]{2,1,0:T(8,128)(2,1)} %get-tuple-element.32.own_ref, s32[8,8,128]{2,1,0:T(8,128)} %get-tuple-element.33.lists_ref), custom_call_target="tpu_custom_call" | custom-call | tf_op jit(solution)/shard_map/first/pallas_call | solution.py:753
  50.1 0.9 copy-done.1
  51.0 1.0 copy-done.3
  52.0 0.9 copy-done.7
  53.0 23.8 %batch0.1 = (f32[1024,172]{1,0:T(8,128)S(1)}, bf16[6,256,128]{2,1,0:T(8,128)(2,1)S(1)}, bf16[32,16,128]{2,1,0:T(8,128)(2,1)S(1)}) custom-call(s32[2,128,33]{2,1,0:T(8,128)S(1)} %copy.40.nodes_smem, s32[8192]{0:T(1024)S(1)} %copy-done.10, s32[32,8,128]{2,1,0:T(8,128)S(1)} %copy-done.1, bf16[8,6,256,128]{3,2,1,0:T(8,128)(2,1)} %get-tuple-element.35.table_ref, ...), custom_call_target="tpu_custom_call" | custom-call | tf_op jit(solution)/shard_map/batch0/pallas_call | solution.py:772
  76.8 1.0 copy-done.5
  77.7 0.7 copy-done.9
  78.5 0.7 copy-done.12
  79.1 38.9 %second.1 = (bf16[8,6,256,128]{3,2,1,0:T(8,128)(2,1)}, f32[32,16,128]{2,1,0:T(8,128)}) custom-call(bf16[6,256,128]{2,1,0:T(8,128)(2,1)} %copy-done.9, bf16[32,16,128]{2,1,0:T(8,128)(2,1)} %copy-done.12), custom_call_target="tpu_custom_call" | custom-call | tf_op jit(solution)/shard_map/second/pallas_call | solution.py:816
  118.0 2.1 %update.1 = (f32[776,128]{1,0:T(8,128)}, f32[1,128]{1,0:T(1,128)}) custom-call(f32[32,16,128]{2,1,0:T(8,128)} %get-tuple-element.42.total_ref, f32[776,128]{1,0:T(8,128)} %get-tuple-element.37.params_ref.old_ref), custom_call_target="tpu_custom_call" | custom-call | tf_op jit(solution)/shard_map/update/pallas_call | solution.py:825
  120.1 1.0 copy-done.4
  121.1 1.2 copy-done.6
  122.3 24.1 %batch1.1 = (f32[1024,172]{1,0:T(8,128)S(1)}, bf16[32,16,128]{2,1,0:T(8,128)(2,1)S(1)}) custom-call(s32[2,128,33]{2,1,0:T(8,128)S(1)} %copy.40.nodes_smem, s32[8192]{0:T(1024)S(1)} %copy-done.10, s32[32,8,128]{2,1,0:T(8,128)S(1)} %copy-done.2, bf16[8,6,256,128]{3,2,1,0:T(8,128)(2,1)} %get-tuple-element.40.table_ref, s32[32,8,128]{2,1,0:T(8,128)S(1)} %copy-done.2, ...), custom_call_target="tpu_custom_call" | custom-call | tf_op jit(solution)/shard_map/batch1/pallas_call | solution.py:772
  146.5 0.6 copy-done.11
  147.1 1.2 copy.41
  148.3 20.9 %third.1.total_ref = f32[32,16,128]{2,1,0:T(8,128)} custom-call(bf16[32,16,128]{2,1,0:T(8,128)(2,1)} %copy-done.11), custom_call_target="tpu_custom_call" | custom-call | tf_op jit(solution)/shard_map/third/pallas_call | solution.py:795
  169.2 2.1 %final.1 = (f32[1,128]{1,0:T(1,128)}, f32[172,100]{1,0:T(8,128)}, f32[172,100]{1,0:T(8,128)}, f32[1,100]{1,0:T(1,128)}, f32[200,100]{1,0:T(8,128)}, /*index=5*/f...) custom-call(f32[32,16,128]{2,1,0:T(8,128)} %third.1.total_ref, f32[776,128]{1,0:T(8,128)} %get-tuple-element.43.params_ref.old_ref), custom_call_target="tpu_custom_call" | custom-call | tf_op jit(solution)/shard_map/final/pallas_call | solution.py:804
  171.2 1.2 pad_maximum_fusion
  (29 shorter events, 0.2 us)
Async XLA Ops:
  0.6 8.1 %copy-start.15 = (bf16[444,516]{0,1:T(8,128)(2,1)S(1)}, bf16[444,516]{0,1:T(8,128)(2,1)}, u32[]{:S(2)}) copy-start(bf16[444,516]{0,1:T(8,128)(2,1)} %param.25) | copy-start | bytes 1374628
  8.9 1.1 copy-start.14
  10.1 40.0 %copy-start.10 = (s32[8192]{0:T(1024)S(1)}, s32[8192]{0:T(1024)}, u32[]{:S(2)}) copy-start(s32[8192]{0:T(1024)} %slot_smem.3) | copy-start | bytes 98308
  10.1 40.0 %copy-start.13 = (s32[2,128]{1,0:T(2,128)S(1)}, s32[2,128]{1,0:T(2,128)}, u32[]{:S(2)}) copy-start(s32[2,128]{1,0:T(2,128)} %valid_ref.3) | copy-start | bytes 3076
  11.4 38.8 %copy-start = (f32[1024,172]{1,0:T(8,128)S(1)}, f32[1024,172]{1,0:T(8,128)}, u32[]{:S(2)}) copy-start(f32[1024,172]{1,0:T(8,128)} %copy.34.memory_ref) | copy-start | bytes 2113540
  50.1 0.9 copy-start.1
  51.0 1.0 copy-start.3
  52.0 0.9 copy-start.7
  53.0 67.1 %copy-start.2 = (s32[32,8,128]{2,1,0:T(8,128)S(1)}, s32[32,8,128]{2,1,0:T(8,128)}, u32[]{:S(2)}) copy-start(s32[32,8,128]{2,1,0:T(8,128)} %get-tuple-element.34.lists_smem.lists_ref) | copy-start | bytes 393220
  53.0 67.1 %copy-start.8 = (bf16[1024,128]{1,0:T(8,128)(2,1)S(1)}, bf16[1024,128]{1,0:T(8,128)(2,1)}, u32[]{:S(2)}) copy-start(bf16[1024,128]{1,0:T(8,128)(2,1)} %get-tuple-element.36.codes_ref) | copy-start | bytes 786436
  76.7 1.0 copy-start.5
  77.7 0.7 copy-start.9
  78.5 0.7 copy-start.12
  120.1 1.0 copy-start.4
  121.1 1.2 copy-start.6
  146.4 0.6 copy-start.11
  147.1 24.1 %copy-start.16 = (f32[1,128]{1,0:T(1,128)S(1)}, f32[1,128]{1,0:T(1,128)}, u32[]{:S(2)}) copy-start(f32[1,128]{1,0:T(1,128)} %get-tuple-element.45) | copy-start | bytes 1540

commit v2 on v1

--- a/solution.py
+++ b/solution.py
@@ -127,6 +127,9 @@
     pl.semaphore_wait(barrier, devices - 1)
 
 
+BLOCKS = 6
+
+
 class Gather:
     def __init__(self, owners, own_ref, table_ref, send_sem, recv_sem, local_sem):
         self.outer = owners // 2
@@ -138,77 +141,157 @@
         self.own, self.table = own_ref, table_ref
         self.send_sem, self.recv_sem = send_sem, recv_sem
         self.local = pltpu.make_async_copy(own_ref, table_ref.at[mem], local_sem)
-        self.sent = []
-
-    def push(self, shard, block, target, from_own=False):
+        self.sent = 0
+        base = BLOCKS * self.c
+        self.line_first = [base + 2 * self.u, base + 2 * self.u + 1, base + 4]
+        self.pair_first = base + 5
+        self.planes = [base + 2 * (1 - self.u), base + 2 * (1 - self.u) + 1]
+        self.ahead = (jnp.minimum(mem + 2, owners - 1), rep)
+        self.behind = (jnp.maximum(mem - 2, 0), rep)
+        self.beside = (2 * self.a + 1 - self.b, rep)
+        self.plane = (mem, 2 * (1 - self.u) + self.c)
+        self.core = (mem, 2 * self.u + 1 - self.c)
+        self.checks = []
+
+    def push(self, shard, block, target, from_own=False, when=None):
+        index = self.sent
+        self.sent += 1
         src = self.own.at[block] if from_own else self.table.at[shard, block]
-        copy = pltpu.make_async_remote_copy(
-            src_ref=src,
-            dst_ref=self.table.at[shard, block],
-            send_sem=self.send_sem.at[len(self.sent)],
-            recv_sem=self.recv_sem.at[shard, block],
-            device_id=target,
-            device_id_type=MESH_ID,
-        )
-        copy.start()
-        self.sent.append(copy)
+
+        def go():
+            pltpu.make_async_remote_copy(
+                src_ref=src,
+                dst_ref=self.table.at[shard, block],
+                send_sem=self.send_sem.at[index],
+                recv_sem=self.recv_sem.at[shard, block],
+                device_id=target,
+                device_id_type=MESH_ID,
+            ).start()
+
+        self.guard(when, go)
+        self.checks.append((index, when))
+
+    def guard(self, when, go):
+        if when is None:
+            go()
+        else:
+            pl.when(when)(go)
 
     def arrived(self, shard, block):
-        pltpu.make_async_copy(
-            self.table.at[shard, block], self.table.at[shard, block], self.recv_sem.at[shard, block]
-        ).wait()
+        ref = self.table.at[shard, block]
+        pltpu.make_async_copy(ref, ref, self.recv_sem.at[shard, block]).wait()
+
+    def along(self, shard, block, from_own=False):
+        self.push(shard, block, self.ahead, from_own, self.a < self.outer - 1)
+        self.push(shard, block, self.behind, from_own, self.a > 0)
 
     def begin(self):
         self.local.start()
-        a, b, u, c, rep = self.a, self.b, self.u, self.c, self.rep
-        mine = (3 * c + u, 3 * c + 2)
-        self.mine = mine
-        for block in mine:
-            self.push(self.mem, block, (2 * a + 1 - b, rep), True)
-            for d in range(1, self.outer):
-                self.push(self.mem, block, (2 * lax.rem(a + d, self.outer) + b, rep), True)
+        self.push(self.mem, self.pair_first, self.beside, True)
+        for block in self.line_first:
+            self.along(self.mem, block, True)
+            self.push(self.mem, block, self.beside, True)
+        self.along(self.mem, self.pair_first, True)
+
+    def shard(self, t, other):
+        at = jnp.clip(self.a + t, 0, self.outer - 1)
+        return 2 * at + (1 - self.b if other else self.b)
+
+    def take(self, t, other, k):
+        shard = self.shard(t, other)
+        block = self.line_first[k] if k < 3 else self.pair_first
+        onward = (t != 0) and not (other and k < 3)
+
+        there = None
+        if t < 0:
+            there = self.a >= -t
+        if t > 0:
+            there = self.a < self.outer - t
+
+        def also(extra):
+            return extra if there is None else there & extra
+
+        self.guard(there, lambda: self.arrived(shard, block))
+        if t == 0 and k == 3:
+            self.along(shard, block)
+        if onward and t < 0:
+            self.push(shard, block, self.ahead, when=also(self.a < self.outer - 1))
+        if onward and t > 0:
+            self.push(shard, block, self.behind, when=also(self.a > 0))
+        if not other and k < 3:
+            self.push(shard, block, self.beside, when=there)
+        if k < 2:
+            self.push(shard, block, self.plane, when=there)
+        self.push(shard, block, self.core, when=there)
+
+    def from_plane(self, t, other, k):
+        shard, block = self.shard(t, other), self.planes[k]
+        there = None
+        if t < 0:
+            there = self.a >= -t
+        if t > 0:
+            there = self.a < self.outer - t
+        self.guard(there, lambda: self.arrived(shard, block))
+        self.push(shard, block, self.core, when=there)
+
+    def from_core(self, t, other):
+        shard = self.shard(t, other)
+        there = None
+        if t < 0:
+            there = self.a >= -t
+        if t > 0:
+            there = self.a < self.outer - t
+
+        def go():
+            for k in range(BLOCKS):
+                self.arrived(shard, BLOCKS * (1 - self.c) + k)
+
+        self.guard(there, go)
 
     def steps(self):
-        a, b, u, c, rep, mem = self.a, self.b, self.u, self.c, self.rep, self.mem
-        beside_x = (2 * a + 1 - b, rep)
-        beside_y = (mem, 2 * (1 - u) + c)
-        beside_core = (mem, 2 * u + 1 - c)
-        order = [(0, 1)]
-        for d in range(1, self.outer):
-            order.append((d, 0))
-        for d in range(1, self.outer):
-            order.append((d, 1))
-        shards = []
-        for d, other in order:
-            shards.append((2 * lax.rem(a + d, self.outer) + (1 - b if other else b), other))
-        for shard, other in shards:
-            for k, block in enumerate(self.mine):
-                self.arrived(shard, block)
-                if not other:
-                    self.push(shard, block, beside_x)
-                if k == 0:
-                    self.push(shard, block, beside_y)
-                self.push(shard, block, beside_core)
+        far = self.outer - 1
+        self.take(0, True, 3)
+        for k in range(3):
+            for t in (-1, 1):
+                self.take(t, False, k)
+            self.take(0, True, k)
+            yield
+        for t in range(1, far + 1):
+            for k in range(3):
+                for s in (-t, t):
+                    self.take(s, True, k)
+                    if t < far:
+                        self.take(s + (1 if s > 0 else -1), False, k)
                 yield
-        for shard, _ in shards:
-            block = 3 * c + 1 - u
-            self.arrived(shard, block)
-            self.push(shard, block, beside_core)
+            for s in (-t, t):
+                self.take(s, False, 3)
+                self.take(s, True, 3)
+            if t == 1:
+                self.from_plane(0, True, 0)
+                self.from_plane(0, True, 1)
             yield
-        for shard, _ in shards:
-            for k in range(3):
-                self.arrived(shard, 3 * (1 - c) + k)
+            for s in (-t, t):
+                for k in range(2):
+                    self.from_plane(s, False, k)
+                    self.from_plane(s, True, k)
             yield
+        self.from_core(0, True)
+        for t in range(1, far + 1):
+            for s in (-t, t):
+                self.from_core(s, False)
+                self.from_core(s, True)
 
     def finish(self):
-        for copy in self.sent:
-            copy.wait_send()
+        for index, when in self.checks:
+            ref = self.own.at[0]
+            copy = pltpu.make_async_copy(ref, ref, self.send_sem.at[index])
+            self.guard(when, copy.wait)
         self.local.wait()
 
 
 def gather_sends(owners):
     outer = owners // 2
-    return 2 * outer + 2 * (outer - 1) + 4 * (owners - 1)
+    return 12 + 16 * outer + 4 * BLOCKS * owners
 
 
 class Exchange:
@@ -457,10 +540,10 @@
     base = shard * 4 * quarter
     lane = iota((quarter, LANES), 1)
     for c in range(2):
-        for u in range(2):
-            at = pl.multiple_of(base + (2 * c + u) * quarter, quarter)
-            low_ref[pl.ds(at, quarter), :] = table_ref[shard, 3 * c + u].astype(F32)
-        both = table_ref[shard, 3 * c + 2].astype(F32)
+        at = pl.multiple_of(base + 2 * c * quarter, quarter)
+        low = table_ref[shard, BLOCKS * c : BLOCKS * c + 4].astype(F32)
+        low_ref[pl.ds(at, 2 * quarter), :] = low.reshape(2 * quarter, LANES)
+        both = table_ref[shard, BLOCKS * c + 4 : BLOCKS * c + 6].astype(F32).reshape(quarter, LANES)
         at = pl.multiple_of(base + 2 * c * quarter, quarter)
         high_ref[pl.ds(at, quarter), :] = jnp.where(lane < LANES // 2, both, 0.0)
         at = pl.multiple_of(base + (2 * c + 1) * quarter, quarter)
@@ -565,12 +648,14 @@
         out_ref[rows, LANES:width] = new_high[:, :rest]
         if blocks_ref is not None:
             c, u = q // 2, q % 2
-            blocks_ref[3 * c + u] = new_low.astype(BF)
+            at = BLOCKS * c + 2 * u
+            blocks_ref[at : at + 2] = new_low.astype(BF).reshape(2, quarter // 2, LANES)
             masked = jnp.where(lane < rest, new_high, 0.0)
             if u == 0:
                 held = masked
             else:
-                blocks_ref[3 * c + 2] = (held + pltpu.roll(masked, LANES // 2, 1)).astype(BF)
+                both = (held + pltpu.roll(masked, LANES // 2, 1)).astype(BF)
+                blocks_ref[BLOCKS * c + 4 : BLOCKS * c + 6] = both.reshape(2, quarter // 2, LANES)
 
 
 def loss_step(pack, batch, neighbours, params_ref, valid_ref, own_low, own_high, nbr_low, nbr_high, table_ref, out_ref):
@@ -649,13 +734,16 @@
     for c in range(2):
         for u in range(2):
             rows = slice((2 * c + u) * quarter, (2 * c + u + 1) * quarter)
-            blocks_ref[3 * c + u] = memory_ref[rows, 0:LANES].astype(BF)
+            at = BLOCKS * c + 2 * u
+            low = memory_ref[rows, 0:LANES].astype(BF)
+            blocks_ref[at : at + 2] = low.reshape(2, quarter // 2, LANES)
         first = slice(2 * c * quarter, (2 * c + 1) * quarter)
         second = slice((2 * c + 1) * quarter, (2 * c + 2) * quarter)
-        blocks_ref[3 * c + 2] = (
+        both = (
             pad_lanes(memory_ref[first, LANES:width])
             + pltpu.roll(pad_lanes(memory_ref[second, LANES:width]), LANES // 2, 1)
         ).astype(BF)
+        blocks_ref[BLOCKS * c + 4 : BLOCKS * c + 6] = both.reshape(2, quarter // 2, LANES)
 
 
 def batch_kernel(batch, last, cap, code, pack, nodes_smem, slot_smem, lists_smem, table_ref, lists_ref, codes_ref, memory_ref, valid_ref, gi_ref, gh_ref, bias_ref, params_ref, *refs):
@@ -714,7 +802,7 @@
             sds((owners, 8, 2 * cap), jnp.int32),
             sds((stamps, LANES), BF),
             sds((pack.rows, LANES), F32),
-            sds((6, quarter, LANES), BF),
+            sds((2 * BLOCKS, quarter // 2, LANES), BF),
         ),
         in_specs=vmem(13),
         out_specs=tuple(vmem(4)),
@@ -739,7 +827,7 @@
 
     dma = pltpu.SemaphoreType.DMA
     sends = gather_sends(owners)
-    gather_sems = [dma((sends,)), dma((owners, 6)), dma((2,))]
+    gather_sems = [dma((sends,)), dma((owners, 2 * BLOCKS)), dma((2,))]
     reduce_scratch = [
         pltpu.VMEM((devices, 16, LANES), BF),
         pltpu.VMEM((16, LANES), F32),
@@ -748,7 +836,7 @@
         dma((devices,)),
         dma((devices,)),
     ]
-    table_shape = sds((owners, 6, quarter, LANES), BF)
+    table_shape = sds((owners, 2 * BLOCKS, quarter // 2, LANES), BF)
     total_shape = sds((devices, 16, LANES), F32)
     table, all_lists = pl.pallas_call(
         functools.partial(first_kernel, owners, reps),
@@ -765,7 +853,7 @@
         last = batch == batches - 1
         outs = [sds((node_dev, width), F32)]
         if not last:
-            outs.append(sds((6, quarter, LANES), BF))
+            outs.append(sds((2 * BLOCKS, quarter // 2, LANES), BF))
         outs.append(sds((devices, 16, LANES), BF))
         letters = devices * cap
         slots = node_slot.shape[0]
@@ -1062,6 +1150,7 @@
         shaped = (
             reps == 4
             and owners % 2 == 0
+            and owners > 4
             and batches == 2
             and 2 * cap == LANES
             and events == LANES

time: 174 us -> 165 us (0.948)
  Pallas kernels: 151 us -> 143 us
    pallas_call x1, Pallas kernels: 38.9 us -> 33.9 us  [quick_body(): pl.pallas_call(functools.partial(second_kernel, owners, reps), out_shape=...]
    pallas_call x1, Pallas kernels: 20.9 us -> 19 us  [quick_body(): pl.pallas_call(functools.partial(third_kernel, owners, reps), out_shape=t...]
where the time goes in v2:
time: 165 us
  Pallas kernels  143 us (87%)
  local copies, waits for them, and re-layouts  19 us (12%)
    pallas_call x2, Pallas kernels, quick_body(): pl.pallas_call(functools.partial(batch_kernel, batch, last, cap, code, pa...  47.7 us
    pallas_call x1, Pallas kernels, quick_body(): pl.pallas_call(functools.partial(second_kernel, owners, reps), out_shape=...  33.9 us
    pallas_call x1, Pallas kernels, quick_body(): pl.pallas_call(functools.partial(first_kernel, owners, reps), out_shape=(...  33 us
    pallas_call x1, Pallas kernels, quick_body(): pl.pallas_call(functools.partial(third_kernel, owners, reps), out_shape=t...  19 us
    unnamed x37, local copies, waits for them, and re-layouts  12 us
    pallas_call x1, Pallas kernels, quick_body(): pl.pallas_call(functools.partial(start_kernel, owners, node_dev, cap, cod...  4.81 us

profile of v2, /device:TPU:0, one launch (start us, length us, event | category | flops | bytes accessed | tf_op | source)
XLA Modules:
  0.0 164.5 jit_solution(1035425004230634953)
XLA Ops:
  1.4 1.2 pad_bitcast_fusion
  2.5 1.3 broadcast_in_dim.24
  3.8 0.7 slice_bitcast_fusion
  4.5 0.6 copy.33
  5.1 0.8 reshape.57
  5.8 0.8 reshape.58
  6.6 0.9 copy.40.nodes_smem
  7.5 1.2 reshape.63
  8.8 0.2 reshape.55
  8.9 0.3 copy.35
  9.3 0.1 fusion.5.gi_ref
  9.5 0.6 copy-done.14
  10.1 1.3 copy.34.memory_ref
  11.4 4.8 %start.1 = (s32[8,8,128]{2,1,0:T(8,128)}, bf16[1024,128]{1,0:T(8,128)(2,1)}, f32[776,128]{1,0:T(8,128)}, bf16[12,128,128]{2,1,0:T(8,128)(2,1)}) custom-call(s32[64,128]{1,0:T(8,128)} %bitcast.28, s32[1,512]{1,0:T(1,128)} %bitcast.33, s32[1,512]{1,0:T(1,128)} %bitcast.32, f32[1,128]{1,0:T(1,128)} %get-tuple-element.76.freq_ref, ...), custom_call_target="tpu_custom_call" | custom-call | tf_op jit(solution)/shard_map/start/pallas_call | solution.py:799
  16.2 33.0 %first.1 = (bf16[8,12,128,128]{3,2,1,0:T(8,128)(2,1)}, s32[32,8,128]{2,1,0:T(8,128)}) custom-call(bf16[12,128,128]{2,1,0:T(8,128)(2,1)} %get-tuple-element.32.own_ref, s32[8,8,128]{2,1,0:T(8,128)} %get-tuple-element.33.lists_ref), custom_call_target="tpu_custom_call" | custom-call | tf_op jit(solution)/shard_map/first/pallas_call | solution.py:841
  49.2 0.9 copy-done.1
  50.1 1.0 copy-done.3
  51.1 0.9 copy-done.7
  52.1 23.8 %batch0.1 = (f32[1024,172]{1,0:T(8,128)S(1)}, bf16[12,128,128]{2,1,0:T(8,128)(2,1)S(1)}, bf16[32,16,128]{2,1,0:T(8,128)(2,1)S(1)}) custom-call(s32[2,128,33]{2,1,0:T(8,128)S(1)} %copy.40.nodes_smem, s32[8192]{0:T(1024)S(1)} %copy-done.10, s32[32,8,128]{2,1,0:T(8,128)S(1)} %copy-done.1, bf16[8,12,128,128]{3,2,1,0:T(8,128)(2,1)} %get-tuple-element.35.table_ref, ...), custom_call_target="tpu_custom_call" | custom-call | tf_op jit(solution)/shard_map/batch0/pallas_call | solution.py:860
  75.8 1.0 copy-done.5
  76.8 0.7 copy-done.9
  77.6 0.7 copy-done.12
  78.2 33.9 %second.1 = (bf16[8,12,128,128]{3,2,1,0:T(8,128)(2,1)}, f32[32,16,128]{2,1,0:T(8,128)}) custom-call(bf16[12,128,128]{2,1,0:T(8,128)(2,1)} %copy-done.9, bf16[32,16,128]{2,1,0:T(8,128)(2,1)} %copy-done.12), custom_call_target="tpu_custom_call" | custom-call | tf_op jit(solution)/shard_map/second/pallas_call | solution.py:904
  112.1 2.1 %update.1 = (f32[776,128]{1,0:T(8,128)}, f32[1,128]{1,0:T(1,128)}) custom-call(f32[32,16,128]{2,1,0:T(8,128)} %get-tuple-element.42.total_ref, f32[776,128]{1,0:T(8,128)} %get-tuple-element.37.params_ref.old_ref), custom_call_target="tpu_custom_call" | custom-call | tf_op jit(solution)/shard_map/update/pallas_call | solution.py:913
  114.3 1.0 copy-done.4
  115.2 1.2 copy-done.6
  116.5 23.9 %batch1.1 = (f32[1024,172]{1,0:T(8,128)S(1)}, bf16[32,16,128]{2,1,0:T(8,128)(2,1)S(1)}) custom-call(s32[2,128,33]{2,1,0:T(8,128)S(1)} %copy.40.nodes_smem, s32[8192]{0:T(1024)S(1)} %copy-done.10, s32[32,8,128]{2,1,0:T(8,128)S(1)} %copy-done.2, bf16[8,12,128,128]{3,2,1,0:T(8,128)(2,1)} %get-tuple-element.40.table_ref, s32[32,8,128]{2,1,0:T(8,128)S(1)} %copy-done.2, ...), custom_call_target="tpu_custom_call" | custom-call | tf_op jit(solution)/shard_map/batch1/pallas_call | solution.py:860
  140.4 0.6 copy-done.11
  141.0 1.2 copy.41
  142.2 19.0 %third.1.total_ref = f32[32,16,128]{2,1,0:T(8,128)} custom-call(bf16[32,16,128]{2,1,0:T(8,128)(2,1)} %copy-done.11), custom_call_target="tpu_custom_call" | custom-call | tf_op jit(solution)/shard_map/third/pallas_call | solution.py:883
  161.2 2.1 %final.1 = (f32[1,128]{1,0:T(1,128)}, f32[172,100]{1,0:T(8,128)}, f32[172,100]{1,0:T(8,128)}, f32[1,100]{1,0:T(1,128)}, f32[200,100]{1,0:T(8,128)}, /*index=5*/f...) custom-call(f32[32,16,128]{2,1,0:T(8,128)} %third.1.total_ref, f32[776,128]{1,0:T(8,128)} %get-tuple-element.43.params_ref.old_ref), custom_call_target="tpu_custom_call" | custom-call | tf_op jit(solution)/shard_map/final/pallas_call | solution.py:892
  163.3 1.2 pad_maximum_fusion
  (29 shorter events, 0.2 us)
Async XLA Ops:
  0.6 8.1 %copy-start.15 = (bf16[444,516]{0,1:T(8,128)(2,1)S(1)}, bf16[444,516]{0,1:T(8,128)(2,1)}, u32[]{:S(2)}) copy-start(bf16[444,516]{0,1:T(8,128)(2,1)} %param.25) | copy-start | bytes 1374628
  8.9 1.1 copy-start.14
  10.1 39.1 %copy-start.10 = (s32[8192]{0:T(1024)S(1)}, s32[8192]{0:T(1024)}, u32[]{:S(2)}) copy-start(s32[8192]{0:T(1024)} %slot_smem.3) | copy-start | bytes 98308
  10.1 39.1 %copy-start.13 = (s32[2,128]{1,0:T(2,128)S(1)}, s32[2,128]{1,0:T(2,128)}, u32[]{:S(2)}) copy-start(s32[2,128]{1,0:T(2,128)} %valid_ref.3) | copy-start | bytes 3076
  11.4 37.9 %copy-start = (f32[1024,172]{1,0:T(8,128)S(1)}, f32[1024,172]{1,0:T(8,128)}, u32[]{:S(2)}) copy-start(f32[1024,172]{1,0:T(8,128)} %copy.34.memory_ref) | copy-start | bytes 2113540
  49.2 0.9 copy-start.1
  50.1 1.0 copy-start.3
  51.1 0.9 copy-start.7
  52.1 62.2 %copy-start.2 = (s32[32,8,128]{2,1,0:T(8,128)S(1)}, s32[32,8,128]{2,1,0:T(8,128)}, u32[]{:S(2)}) copy-start(s32[32,8,128]{2,1,0:T(8,128)} %get-tuple-element.34.lists_smem.lists_ref) | copy-start | bytes 393220
  52.1 62.2 %copy-start.8 = (bf16[1024,128]{1,0:T(8,128)(2,1)S(1)}, bf16[1024,128]{1,0:T(8,128)(2,1)}, u32[]{:S(2)}) copy-start(bf16[1024,128]{1,0:T(8,128)(2,1)} %get-tuple-element.36.codes_ref) | copy-start | bytes 786436
  75.8 1.0 copy-start.5
  76.8 0.7 copy-start.9
  77.6 0.7 copy-start.12
  114.2 1.0 copy-start.4
  115.2 1.2 copy-start.6
  140.4 0.6 copy-start.11
  141.0 22.3 %copy-start.16 = (f32[1,128]{1,0:T(1,128)S(1)}, f32[1,128]{1,0:T(1,128)}, u32[]{:S(2)}) copy-start(f32[1,128]{1,0:T(1,128)} %get-tuple-element.45) | copy-start | bytes 1540

commit v3 on v2

--- a/solution.py
+++ b/solution.py
@@ -50,9 +50,12 @@
     return jnp.concatenate([x, jnp.zeros((rows - x.shape[0], x.shape[1]), x.dtype)], 0)
 
 
-def lists_kernel(owners, node_dev, cap, width, slot_ref, pair_ref, time_ref, freq_ref, phase_ref, lists_ref, codes_ref):
+def make_lists(owners, node_dev, cap, slot_ref, nodes_ref, time_ref, lists_ref):
     groups = slot_ref.shape[0]
-    ids = pair_ref[...]
+    ids = []
+    for b in range(2):
+        ids += [nodes_ref[0, b : b + 1], nodes_ref[1, b : b + 1]]
+    ids = jnp.concatenate(ids, 1)
     letters = ids.shape[1]
     per_batch = letters // 2
     grid = slot_ref[...]
@@ -85,7 +88,7 @@
     rank = jnp.sum(before * owner_hot, 0, keepdims=True).astype(jnp.int32)
     batch = iota((1, letters), 1) // per_batch
     seat = owner * (2 * cap) + batch * cap + rank
-    times = time_ref[...]
+    times = jnp.concatenate([time_ref[0:1], time_ref[0:1], time_ref[1:2], time_ref[1:2]], 1)
     values = jnp.concatenate(
         [
             offset >> 8, offset & 255, partners >> 8, partners & 255,
@@ -103,28 +106,18 @@
             placed[4:5] * 256.0 + placed[5:6],
         ]
         lists_ref[o] = jnp.concatenate(rows + [jnp.zeros((5, 2 * cap), F32)], 0).astype(jnp.int32)
+
+
+def make_codes(width, pad_ref, codes_ref):
     stamps = iota(codes_ref.shape, 0).astype(F32)
-    code = jnp.cos(stamps * freq_ref[...] + phase_ref[...])
     lane = iota(codes_ref.shape, 1)
+    code = jnp.cos(stamps * pad_ref[0:1] + pad_ref[1:2])
     code = jnp.where(lane < width, code, jnp.where(lane == width, 1.0, 0.0))
     codes_ref[...] = code.astype(BF)
 
 
 def peer(index, reps):
     return (index // reps, lax.rem(index, reps))
-
-
-def enter(devices, reps, me):
-    barrier = pltpu.get_barrier_semaphore()
-
-    def greet(k, carry):
-        pl.semaphore_signal(
-            barrier, inc=1, device_id=peer(lax.rem(me + k, devices), reps), device_id_type=MESH_ID
-        )
-        return carry
-
-    lax.fori_loop(1, devices, greet, 0)
-    pl.semaphore_wait(barrier, devices - 1)
 
 
 BLOCKS = 6
@@ -275,6 +268,7 @@
                     self.from_plane(s, False, k)
                     self.from_plane(s, True, k)
             yield
+        self.local.wait()
         self.from_core(0, True)
         for t in range(1, far + 1):
             for s in (-t, t):
@@ -286,7 +280,6 @@
             ref = self.own.at[0]
             copy = pltpu.make_async_copy(ref, ref, self.send_sem.at[index])
             self.guard(when, copy.wait)
-        self.local.wait()
 
 
 def gather_sends(owners):
@@ -335,30 +328,7 @@
         lax.fori_loop(1, self.devices, one, 0)
 
 
-def first_kernel(owners, reps, own_ref, lists_ref, table_ref, all_lists_ref, send_sem, recv_sem, local_sem, ls, lr):
-    me = lax.axis_index("mem") * reps + lax.axis_index("rep")
-    devices = owners * reps
-    enter(devices, reps, me)
-    gather = Gather(owners, own_ref, table_ref, send_sem, recv_sem, local_sem.at[0])
-    lists = Exchange(
-        devices, reps, me,
-        lambda to: lists_ref.at[to // reps], lambda come: all_lists_ref.at[come], ls, lr,
-    )
-    mine = pltpu.make_async_copy(
-        lists_ref.at[lax.axis_index("mem")], all_lists_ref.at[me], local_sem.at[1]
-    )
-    lists.start()
-    mine.start()
-    gather.begin()
-    for _ in gather.steps():
-        pass
-    lists.wait_recv()
-    lists.wait_send()
-    mine.wait()
-    gather.finish()
-
-
-def reduce_parts(devices, reps, me, grads_ref, parts_ref, sum_ref, total_ref, sems, between=None):
+def reduce_parts(devices, reps, me, grads_ref, parts_ref, sum_ref, total_ref, sems):
     scatter = Exchange(
         devices, reps, me, lambda to: grads_ref.at[to], lambda come: parts_ref.at[come],
         sems[0], sems[1],
@@ -374,39 +344,6 @@
     total = jnp.sum(parts_ref[...].astype(F32), 0)
     sum_ref[...] = total
     total_ref[me] = total
-
-
-def second_kernel(owners, reps, own_ref, grads_ref, table_ref, total_ref, send_sem, recv_sem, local_sem, parts_ref, sum_ref, s0, s1, s2, s3):
-    me = lax.axis_index("mem") * reps + lax.axis_index("rep")
-    devices = owners * reps
-    enter(devices, reps, me)
-    gather = Gather(owners, own_ref, table_ref, send_sem, recv_sem, local_sem.at[0])
-    scatter, share = reduce_parts(devices, reps, me, grads_ref, parts_ref, sum_ref, total_ref, (s0, s1, s2, s3))
-    scatter.start()
-    gather.begin()
-    for step, _ in enumerate(gather.steps()):
-        if step == 2:
-            scatter.wait_recv()
-            reduce_middle(me, grads_ref, parts_ref, sum_ref, total_ref)
-            share.start()
-    share.wait_recv()
-    scatter.wait_send()
-    share.wait_send()
-    gather.finish()
-
-
-def third_kernel(owners, reps, grads_ref, total_ref, parts_ref, sum_ref, s0, s1, s2, s3):
-    me = lax.axis_index("mem") * reps + lax.axis_index("rep")
-    devices = owners * reps
-    enter(devices, reps, me)
-    scatter, share = reduce_parts(devices, reps, me, grads_ref, parts_ref, sum_ref, total_ref, (s0, s1, s2, s3))
-    scatter.start()
-    scatter.wait_recv()
-    reduce_middle(me, grads_ref, parts_ref, sum_ref, total_ref)
-    share.start()
-    share.wait_recv()
-    scatter.wait_send()
-    share.wait_send()
 
 
 def up8(n):
@@ -553,9 +490,12 @@
 
 
 def partner_rows(batch, cap, lists_smem, low_ref, high_ref, out_low, out_high):
+    slots = low_ref.shape[0]
+
     def one(d, carry):
         for j in range(cap):
             p = lists_smem[d, 1, batch * cap + j]
+            p = p & (slots - 1) if slots & (slots - 1) == 0 else jnp.clip(p, 0, slots - 1)
             at = d * cap + j
             out_low[pl.ds(at, 1), :] = low_ref[pl.ds(p, 1), :]
             out_high[pl.ds(at, 1), :] = high_ref[pl.ds(p, 1), :]
@@ -564,13 +504,13 @@
     lax.fori_loop(0, lists_smem.shape[0], one, 0)
 
 
-def event_rows(batch, nodes_smem, slot_smem, low_ref, high_ref, own_low, own_high, nbr_low, nbr_high):
-    _, events, columns = nodes_smem.shape
-    neighbours = (columns - 3) // 3
+def event_rows(batch, first, count, nodes_smem, slot_smem, low_ref, high_ref, own_low, own_high, nbr_low, nbr_high):
+    neighbours = (nodes_smem.shape[0] - 3) // 3
+    events = nodes_smem.shape[2]
 
     def one(e, carry):
         def row(col):
-            slot = slot_smem[nodes_smem[batch, e, col]]
+            slot = slot_smem[nodes_smem[col, batch, e]]
             return low_ref[pl.ds(slot, 1), :], high_ref[pl.ds(slot, 1), :]
 
         for r in range(3):
@@ -586,7 +526,7 @@
             nbr_high[at, :] = high
         return carry
 
-    lax.fori_loop(0, events, one, 0)
+    lax.fori_loop(first, first + count, one, 0)
 
 
 def pair_row(batch, cap, lists_ref, i, row):
@@ -632,7 +572,7 @@
         )
         mean = (summed / jnp.maximum(counts, 1.0)).astype(BF)
         low = memory_ref[rows, 0:LANES]
-        high = pad_lanes(memory_ref[rows, LANES:width])
+        high = memory_ref[rows, LANES : 2 * LANES]
         old = jnp.concatenate([low, high], 1)
         state = old.astype(BF)
         joined = jnp.concatenate([state, mean], 1)
@@ -644,9 +584,12 @@
         fresh = (1.0 - update) * candidate + update * old
         new = jnp.where(counts > 0.5, fresh, old)
         new_low, new_high = new[:, :LANES], new[:, LANES:]
-        out_ref[rows, 0:LANES] = new_low
-        out_ref[rows, LANES:width] = new_high[:, :rest]
-        if blocks_ref is not None:
+        if blocks_ref is None:
+            out_ref[0:LANES, rows] = new_low.T
+            out_ref[LANES:width, rows] = new_high.T[:rest]
+        else:
+            out_ref[rows, 0:LANES] = new_low
+            out_ref[rows, LANES : 2 * LANES] = new_high
             c, u = q // 2, q % 2
             at = BLOCKS * c + 2 * u
             blocks_ref[at : at + 2] = new_low.astype(BF).reshape(2, quarter // 2, LANES)
@@ -725,201 +668,326 @@
     pack_grads(pack, (g_s[0], g_s[1], g_n[0], g_n[1], g_top, g_bottom), small, table_ref, out_ref)
 
 
-def start_kernel(owners, node_dev, cap, code, pack, slot_ref, pair_ref, time_ref, freq_ref, phase_ref, memory_ref, *refs):
-    params, (lists_ref, codes_ref, packed_ref, blocks_ref) = refs[:7], refs[7:]
-    lists_kernel(owners, node_dev, cap, code, slot_ref, pair_ref, time_ref, freq_ref, phase_ref, lists_ref, codes_ref)
-    pack_params(pack, params, packed_ref)
-    width = memory_ref.shape[1]
+def turn_memory(turned_ref, memory_ref, blocks_ref):
+    width, node_dev = turned_ref.shape
     quarter = node_dev // 4
-    for c in range(2):
-        for u in range(2):
-            rows = slice((2 * c + u) * quarter, (2 * c + u + 1) * quarter)
-            at = BLOCKS * c + 2 * u
-            low = memory_ref[rows, 0:LANES].astype(BF)
-            blocks_ref[at : at + 2] = low.reshape(2, quarter // 2, LANES)
-        first = slice(2 * c * quarter, (2 * c + 1) * quarter)
-        second = slice((2 * c + 1) * quarter, (2 * c + 2) * quarter)
-        both = (
-            pad_lanes(memory_ref[first, LANES:width])
-            + pltpu.roll(pad_lanes(memory_ref[second, LANES:width]), LANES // 2, 1)
-        ).astype(BF)
-        blocks_ref[BLOCKS * c + 4 : BLOCKS * c + 6] = both.reshape(2, quarter // 2, LANES)
-
-
-def batch_kernel(batch, last, cap, code, pack, nodes_smem, slot_smem, lists_smem, table_ref, lists_ref, codes_ref, memory_ref, valid_ref, gi_ref, gh_ref, bias_ref, params_ref, *refs):
-    if last:
-        (out_ref, grads_ref), rest = refs[:2], refs[2:]
-        blocks_ref = None
-    else:
-        (out_ref, blocks_ref, grads_ref), rest = refs[:3], refs[3:]
-    low, high, p_low, p_high, letters, hot, own_low, own_high, nbr_low, nbr_high, flat = rest
-    owners = table_ref.shape[0]
-    quarter = memory_ref.shape[0] // 4
-    neighbours = (nodes_smem.shape[2] - 3) // 3
-
-    def spread(s, carry):
-        expand(table_ref, low, high, s, quarter)
+    rest = width - LANES
+    held = None
+    for q in range(4):
+        rows = slice(q * quarter, (q + 1) * quarter)
+        c, u = q // 2, q % 2
+        low = turned_ref[0:LANES, rows].T
+        memory_ref[rows, 0:LANES] = low
+        at = BLOCKS * c + 2 * u
+        blocks_ref[at : at + 2] = low.astype(BF).reshape(2, quarter // 2, LANES)
+        pad = jnp.zeros((LANES - up8(rest), quarter), F32)
+        high = turned_ref[LANES:width, rows]
+        if up8(rest) != rest:
+            high = jnp.concatenate([high, jnp.zeros((up8(rest) - rest, quarter), F32)], 0)
+        high = jnp.concatenate([high, pad], 0).T
+        memory_ref[rows, LANES : 2 * LANES] = high
+        if u == 0:
+            held = high
+        else:
+            both = (held + pltpu.roll(high, LANES // 2, 1)).astype(BF)
+            blocks_ref[BLOCKS * c + 4 : BLOCKS * c + 6] = both.reshape(2, quarter // 2, LANES)
+
+
+def pack_turned(width, source_ref, spans, wide_ref, out_ref):
+    rows, columns = source_ref.shape
+    wide_ref[...] = jnp.zeros_like(wide_ref)
+    wide_ref[0:rows, 0:columns] = source_ref[...].astype(F32)
+    total = wide_ref.shape[1]
+    keep = 2 * LANES
+    for j in range(3):
+        part = wide_ref[j * width : j * width + keep, :]
+        for start, size, to in spans:
+            span = -(-size // LANES) * LANES
+            moved = part if start == 0 else pltpu.roll(part, total - start, 1)
+            moved = moved[:, :span]
+            inside = (iota(moved.shape, 1) < size) & (iota(moved.shape, 0) < width)
+            out_ref[j, to : to + span, :] = jnp.where(inside, moved, 0.0).T.astype(BF)
+
+
+def pack_gates(width, source_ref, spans, wide_ref, out_ref):
+    rows, columns = source_ref.shape
+    wide_ref[...] = jnp.zeros_like(wide_ref)
+    wide_ref[0:rows, 0:columns] = source_ref[...].astype(F32)
+    total = wide_ref.shape[1]
+    out_ref[...] = jnp.zeros_like(out_ref)
+    for start, size, to in spans:
+        part = wide_ref[start : start + size, :]
+        for j in range(3):
+            moved = part if j == 0 else pltpu.roll(part, total - j * width, 1)
+            moved = moved[:, : 2 * LANES]
+            moved = jnp.where(iota(moved.shape, 1) < width, moved, 0.0)
+            out_ref[j, to : to + size, :] = moved.astype(BF)
+
+
+def pack_bias(width, in_ref, hid_ref, wide_ref, out_ref):
+    total = wide_ref.shape[1]
+    columns = in_ref.shape[0]
+    wide_ref[0:8, :] = jnp.zeros((8, total), F32)
+    wide_ref[0:1, 0:columns] = in_ref[...].reshape(1, columns)
+    wide_ref[1:2, 0:columns] = hid_ref[...].reshape(1, columns)
+    part = wide_ref[0:8, :]
+    for j in range(3):
+        moved = part if j == 0 else pltpu.roll(part, total - j * width, 1)
+        moved = jnp.where(iota((8, 2 * LANES), 1) < width, moved[:, : 2 * LANES], 0.0)
+        out_ref[j : j + 1] = moved[0:1]
+        out_ref[j + 3 : j + 4] = moved[1:2]
+
+
+def window_kernel(owners, reps, cap, code, pack, *refs):
+    (
+        nodes_smem, slot_smem, nodes_ref, slot_ref, time_ref, valid_ref, freq_ref, phase_ref,
+        turned_ref, gru_in_ref, gru_hid_ref, in_bias_ref, hid_bias_ref,
+    ) = refs[:13]
+    params = refs[13:20]
+    memory_out, loss_ref, packed_out = refs[20:23]
+    (
+        memory_ref, blocks, table, low, high, p_low, p_high, letters, hot, own_low, own_high, nbr_low, nbr_high,
+        flat, middle, lists_ref, all_lists, lists_smem, codes, packed, gi, gh, bias, wide, pad_ref,
+        grads, parts, sums, totals,
+        send_sems, recv_sems, local_sem, list_sems, reduce_sems,
+    ) = refs[23:]
+    me = lax.axis_index("mem") * reps + lax.axis_index("rep")
+    devices = owners * reps
+    width, node_dev = turned_ref.shape
+    quarter = node_dev // 4
+    columns, _, events = nodes_ref.shape
+    neighbours = (columns - 3) // 3
+
+    barrier = pltpu.get_barrier_semaphore()
+
+    def greet(k, carry):
+        pl.semaphore_signal(
+            barrier, inc=1, device_id=peer(lax.rem(me + k, devices), reps), device_id_type=MESH_ID
+        )
         return carry
 
-    lax.fori_loop(0, owners, spread, 0)
-    partner_rows(batch, cap, lists_smem, low, high, p_low, p_high)
-    letters[:, 0:LANES] = p_low[...].astype(BF)
-    letters[:, LANES : 2 * LANES] = p_high[...].astype(BF)
-    letter_codes(batch, cap, lists_ref, codes_ref, letters)
-    memory_step(batch, cap, pack.width, code, lists_ref, letters, memory_ref, gi_ref, gh_ref, bias_ref, hot, out_ref, blocks_ref)
-    event_rows(batch, nodes_smem, slot_smem, low, high, own_low, own_high, nbr_low, nbr_high)
-    loss_step(pack, batch, neighbours, params_ref, valid_ref, own_low, own_high, nbr_low, nbr_high, flat, grads_ref)
-
-
-def update_kernel(pack, total_ref, old_ref, new_ref, loss_ref):
-    loss_ref[...] = update_params(pack, total_ref, old_ref, new_ref)
-
-
-def final_kernel(pack, total_ref, old_ref, *refs):
-    loss_ref, outs, new_ref = refs[0], refs[1:8], refs[8]
-    loss_ref[...] = update_params(pack, total_ref, old_ref, new_ref)
-    unpack_params(pack, new_ref, outs)
+    lax.fori_loop(1, devices, greet, 0)
+    turn_memory(turned_ref, memory_ref, blocks.at[0])
+    pl.semaphore_wait(barrier, devices - 1)
+
+    gathers = [
+        Gather(owners, blocks.at[b], table.at[b], send_sems.at[b], recv_sems.at[b], local_sem.at[b])
+        for b in range(2)
+    ]
+    exchange = Exchange(
+        devices, reps, me,
+        lambda to: lists_ref.at[to // reps], lambda come: all_lists.at[come],
+        list_sems.at[0], list_sems.at[1],
+    )
+    mine = pltpu.make_async_copy(
+        lists_ref.at[lax.axis_index("mem")], all_lists.at[me], local_sem.at[2]
+    )
+    to_smem = pltpu.make_async_copy(all_lists, lists_smem, local_sem.at[3])
+    reduces = [
+        reduce_parts(
+            devices, reps, me, grads.at[b], parts.at[b], sums.at[b], totals.at[b],
+            [reduce_sems.at[4 * b + i] for i in range(4)],
+        )
+        for b in range(2)
+    ]
+
+    gathers[0].begin()
+    make_lists(owners, node_dev, cap, slot_ref, nodes_ref, time_ref, lists_ref)
+    exchange.start()
+    mine.start()
+
+    def time_table():
+        pad_ref[...] = jnp.zeros_like(pad_ref)
+        pad_ref[0:1, 0:code] = freq_ref[...]
+        pad_ref[1:2, 0:code] = phase_ref[...]
+        make_codes(code, pad_ref, codes)
+
+    def lists_in():
+        exchange.wait_recv()
+        mine.wait()
+        to_smem.start()
+
+    def codes_of(batch):
+        return lambda: letter_codes(batch, cap, all_lists, codes, letters.at[batch])
+
+    shadow = [
+        lambda: pack_turned(
+            width, gru_in_ref,
+            [(0, width, 0), (width, width, 2 * LANES), (2 * width, code, 4 * LANES)],
+            wide, gi,
+        ),
+        lambda: pack_gates(width, gru_hid_ref, [(0, width, 0)], wide, gh),
+        lambda: pack_bias(width, in_bias_ref, hid_bias_ref, wide, bias),
+        lambda: pack_params(pack, params, packed.at[0]),
+        time_table,
+        lists_in,
+        codes_of(0),
+        codes_of(1),
+    ]
+    for _ in gathers[0].steps():
+        if shadow:
+            shadow.pop(0)()
+    for task in shadow:
+        task()
+    to_smem.wait()
+
+    def spread(b):
+        def one(s, carry):
+            expand(table.at[b], low, high, s, quarter)
+            return carry
+
+        lax.fori_loop(0, owners, one, 0)
+
+    def partners(b):
+        partner_rows(b, cap, lists_smem, low, high, p_low, p_high)
+        letters[b, :, 0:LANES] = p_low[...].astype(BF)
+        letters[b, :, LANES : 2 * LANES] = p_high[...].astype(BF)
+
+    def remember(b, old_ref, new_ref, blocks_ref):
+        memory_step(
+            b, cap, width, code, all_lists, letters.at[b], old_ref, gi, gh, bias, hot, new_ref, blocks_ref
+        )
+
+    def rows_of(b, first, count):
+        event_rows(
+            b, first, count, nodes_smem, slot_smem, low, high, own_low, own_high, nbr_low, nbr_high
+        )
+
+    def loss_of(b):
+        loss_step(
+            pack, b, neighbours, packed.at[b], valid_ref, own_low, own_high, nbr_low, nbr_high, flat,
+            grads.at[b],
+        )
+
+    spread(0)
+    partners(0)
+    remember(0, memory_ref, middle, blocks.at[1])
+    gathers[1].begin()
+    pieces = 16
+    size = events // pieces
+    tasks = [functools.partial(rows_of, 0, i * size, size) for i in range(pieces)]
+
+    def send_grads():
+        loss_of(0)
+        reduces[0][0].start()
+
+    tasks.append(send_grads)
+    for _ in gathers[1].steps():
+        if tasks:
+            tasks.pop(0)()
+    for task in tasks:
+        task()
+    reduces[0][0].wait_recv()
+    reduce_middle(me, grads.at[0], parts.at[0], sums.at[0], totals.at[0])
+    reduces[0][1].start()
+
+    spread(1)
+    rows_of(1, 0, events)
+    reduces[0][1].wait_recv()
+    loss0 = update_params(pack, totals.at[0], packed.at[0], packed.at[1])
+    loss_of(1)
+    reduces[1][0].start()
+    partners(1)
+    reduces[1][0].wait_recv()
+    reduce_middle(me, grads.at[1], parts.at[1], sums.at[1], totals.at[1])
+    reduces[1][1].start()
+    remember(1, middle, memory_out, None)
+    reduces[1][1].wait_recv()
+    loss1 = update_params(pack, totals.at[1], packed.at[1], packed_out)
+    loss_ref[...] = jnp.where(iota((1, LANES), 1) == 0, loss0, loss1)
+
+    exchange.wait_send()
+    for scatter, share in reduces:
+        scatter.wait_send()
+        share.wait_send()
+    for gather in gathers:
+        gather.finish()
+
+
+def final_kernel(pack, memory_ref, loss_ref, packed_ref, memory_out, loss_out, *outs):
+    memory_out[...] = memory_ref[...]
+    loss_out[...] = loss_ref[0, 0:2]
+    unpack_params(pack, packed_ref, outs)
 
 
 def quick_body(owners, reps, cap, memory, node_slot, event_nodes, event_times, valid_mask, time_freq, time_phase, gru_input, gru_hidden, gru_in_bias, gru_hid_bias, *params):
     node_dev, width = memory.shape
     batches, events, columns = event_nodes.shape
     code = time_freq.shape[0]
-    embed = params[0].shape[1]
     devices = owners * reps
-    pack = Pack(width, embed, devices)
+    pack = Pack(width, params[0].shape[1], devices)
     quarter = node_dev // 4
+    slots = node_slot.shape[0]
+    letters = devices * cap
+    sends = gather_sends(owners)
+    stamps = -(-TIMES // LANES) * LANES
+    wide_rows = up8(2 * width + 2 * LANES)
+    wide_lanes = -(-3 * width // LANES) * LANES + LANES
     sds = jax.ShapeDtypeStruct
-    pairs = event_nodes[:, :, :2].transpose(0, 2, 1).reshape(1, -1)
-    times = jnp.broadcast_to(event_times[:, None, :], (batches, 2, events)).reshape(1, -1)
-    freq = jnp.pad(time_freq, (0, LANES - code))[None, :]
-    phase = jnp.pad(time_phase, (0, LANES - code))[None, :]
+    dma = pltpu.SemaphoreType.DMA
     rows = [p[None, :] if p.ndim == 1 else p for p in params]
-    stamps = -(-TIMES // LANES) * LANES
-    lists, codes, packed, blocks = pl.pallas_call(
-        functools.partial(start_kernel, owners, node_dev, cap, code, pack),
-        out_shape=(
-            sds((owners, 8, 2 * cap), jnp.int32),
-            sds((stamps, LANES), BF),
-            sds((pack.rows, LANES), F32),
-            sds((2 * BLOCKS, quarter // 2, LANES), BF),
+    smem = [pl.BlockSpec(memory_space=pltpu.SMEM)]
+    nodes = event_nodes.transpose(2, 0, 1)
+    made = pl.pallas_call(
+        functools.partial(window_kernel, owners, reps, cap, code, pack),
+        out_shape=(sds((width, node_dev), F32), sds((1, LANES), F32), sds((pack.rows, LANES), F32)),
+        in_specs=smem * 2 + vmem(18),
+        out_specs=tuple(vmem(3)),
+        scratch_shapes=[
+            pltpu.VMEM((node_dev, 2 * LANES), F32),
+            pltpu.VMEM((2, 2 * BLOCKS, quarter // 2, LANES), BF),
+            pltpu.VMEM((2, owners, 2 * BLOCKS, quarter // 2, LANES), BF),
+            pltpu.VMEM((slots, LANES), F32),
+            pltpu.VMEM((slots, LANES), F32),
+            pltpu.VMEM((letters, LANES), F32),
+            pltpu.VMEM((letters, LANES), F32),
+            pltpu.VMEM((2, letters, 3 * LANES), BF),
+            pltpu.VMEM((quarter, letters), BF),
+            pltpu.VMEM((3 * events, LANES), F32),
+            pltpu.VMEM((3 * events, LANES), F32),
+            pltpu.VMEM((3 * events, LANES), F32),
+            pltpu.VMEM((3 * events, LANES), F32),
+            pltpu.VMEM((pack.main, LANES), F32),
+            pltpu.VMEM((node_dev, 2 * LANES), F32),
+            pltpu.VMEM((owners, 8, 2 * cap), jnp.int32),
+            pltpu.VMEM((devices, 8, 2 * cap), jnp.int32),
+            pltpu.SMEM((devices, 8, 2 * cap), jnp.int32),
+            pltpu.VMEM((stamps, LANES), BF),
+            pltpu.VMEM((2, pack.rows, LANES), F32),
+            pltpu.VMEM((3, 5 * LANES, 2 * LANES), BF),
+            pltpu.VMEM((3, 2 * LANES, 2 * LANES), BF),
+            pltpu.VMEM((8, 2 * LANES), F32),
+            pltpu.VMEM((wide_rows, wide_lanes), F32),
+            pltpu.VMEM((8, LANES), F32),
+            pltpu.VMEM((2, devices, 16, LANES), BF),
+            pltpu.VMEM((2, devices, 16, LANES), BF),
+            pltpu.VMEM((2, 16, LANES), F32),
+            pltpu.VMEM((2, devices, 16, LANES), F32),
+            dma((2, sends)),
+            dma((2, owners, 2 * BLOCKS)),
+            dma((4,)),
+            dma((2, devices)),
+            dma((8, devices)),
+        ],
+        compiler_params=pltpu.CompilerParams(
+            collective_id=0, has_side_effects=True, vmem_limit_bytes=56 * 1024 * 1024
         ),
-        in_specs=vmem(13),
-        out_specs=tuple(vmem(4)),
-        name="start",
-    )(node_slot.reshape(-1, LANES), pairs, times, freq, phase, memory, *rows)
-
-    pad_w = 2 * LANES - width
-    gi = gru_input.reshape(-1, 3, width).transpose(1, 0, 2)
-    gi = jnp.concatenate(
-        [
-            jnp.pad(gi[:, :width], ((0, 0), (0, pad_w), (0, pad_w))),
-            jnp.pad(gi[:, width : 2 * width], ((0, 0), (0, pad_w), (0, pad_w))),
-            jnp.pad(gi[:, 2 * width :], ((0, 0), (0, LANES - code), (0, pad_w))),
-        ],
-        1,
-    )
-    gh = jnp.pad(gru_hidden.reshape(width, 3, width).transpose(1, 0, 2), ((0, 0), (0, pad_w), (0, pad_w)))
-    bias = jnp.pad(
-        jnp.concatenate([gru_in_bias.reshape(3, width), gru_hid_bias.reshape(3, width)], 0),
-        ((0, 2), (0, pad_w)),
-    )
-
-    dma = pltpu.SemaphoreType.DMA
-    sends = gather_sends(owners)
-    gather_sems = [dma((sends,)), dma((owners, 2 * BLOCKS)), dma((2,))]
-    reduce_scratch = [
-        pltpu.VMEM((devices, 16, LANES), BF),
-        pltpu.VMEM((16, LANES), F32),
-        dma((devices,)),
-        dma((devices,)),
-        dma((devices,)),
-        dma((devices,)),
-    ]
-    table_shape = sds((owners, 2 * BLOCKS, quarter // 2, LANES), BF)
-    total_shape = sds((devices, 16, LANES), F32)
-    table, all_lists = pl.pallas_call(
-        functools.partial(first_kernel, owners, reps),
-        out_shape=(table_shape, sds((devices, 8, 2 * cap), jnp.int32)),
-        in_specs=vmem(2),
-        out_specs=tuple(vmem(2)),
-        scratch_shapes=gather_sems + [dma((devices,)), dma((devices,))],
-        compiler_params=pltpu.CompilerParams(collective_id=0, has_side_effects=True),
-        name="first",
-    )(blocks, lists)
-
-    losses = []
-    for batch in range(batches):
-        last = batch == batches - 1
-        outs = [sds((node_dev, width), F32)]
-        if not last:
-            outs.append(sds((2 * BLOCKS, quarter // 2, LANES), BF))
-        outs.append(sds((devices, 16, LANES), BF))
-        letters = devices * cap
-        slots = node_slot.shape[0]
-        made = pl.pallas_call(
-            functools.partial(batch_kernel, batch, last, cap, code, pack),
-            out_shape=tuple(outs),
-            in_specs=[pl.BlockSpec(memory_space=pltpu.SMEM)] * 3 + vmem(9),
-            out_specs=tuple(vmem(len(outs))),
-            scratch_shapes=[
-                pltpu.VMEM((slots, LANES), F32),
-                pltpu.VMEM((slots, LANES), F32),
-                pltpu.VMEM((letters, LANES), F32),
-                pltpu.VMEM((letters, LANES), F32),
-                pltpu.VMEM((letters, 3 * LANES), BF),
-                pltpu.VMEM((quarter, letters), BF),
-                pltpu.VMEM((3 * events, LANES), F32),
-                pltpu.VMEM((3 * events, LANES), F32),
-                pltpu.VMEM((3 * events, LANES), F32),
-                pltpu.VMEM((3 * events, LANES), F32),
-                pltpu.VMEM((pack.main, LANES), F32),
-            ],
-            compiler_params=pltpu.CompilerParams(vmem_limit_bytes=48 * 1024 * 1024),
-            name="batch" + str(batch),
-        )(event_nodes, node_slot, all_lists, table, all_lists, codes, memory, valid_mask, gi, gh, bias, packed)
-        if last:
-            memory, grads = made
-            total = pl.pallas_call(
-                functools.partial(third_kernel, owners, reps),
-                out_shape=total_shape,
-                in_specs=vmem(1),
-                out_specs=vmem(1)[0],
-                scratch_shapes=reduce_scratch,
-                compiler_params=pltpu.CompilerParams(collective_id=2, has_side_effects=True),
-                name="third",
-            )(grads)
-            outs = pl.pallas_call(
-                functools.partial(final_kernel, pack),
-                out_shape=(sds((1, LANES), F32),) + tuple(sds(p.shape, F32) for p in rows),
-                in_specs=vmem(2),
-                out_specs=tuple(vmem(8)),
-                scratch_shapes=[pltpu.VMEM((pack.rows, LANES), F32)],
-                name="final",
-            )(total, packed)
-            losses.append(outs[0])
-            params = [o.reshape(p.shape) for o, p in zip(outs[1:], params)]
-        else:
-            memory, blocks, grads = made
-            table, total = pl.pallas_call(
-                functools.partial(second_kernel, owners, reps),
-                out_shape=(table_shape, total_shape),
-                in_specs=vmem(2),
-                out_specs=tuple(vmem(2)),
-                scratch_shapes=gather_sems + reduce_scratch,
-                compiler_params=pltpu.CompilerParams(collective_id=1, has_side_effects=True),
-                name="second",
-            )(blocks, grads)
-            packed, loss = pl.pallas_call(
-                functools.partial(update_kernel, pack),
-                out_shape=(sds((pack.rows, LANES), F32), sds((1, LANES), F32)),
-                in_specs=vmem(2),
-                out_specs=tuple(vmem(2)),
-                name="update",
-            )(total, packed)
-            losses.append(loss)
-    losses = jnp.concatenate([loss[:, 0] for loss in losses])
-    return (memory, losses, *params)
+        name="window",
+    )(
+        nodes, node_slot, nodes, node_slot.reshape(-1, LANES), event_times, valid_mask,
+        time_freq[None, :], time_phase[None, :], memory.T, gru_input.T, gru_hidden,
+        gru_in_bias, gru_hid_bias, *rows,
+    )
+    outs = pl.pallas_call(
+        functools.partial(final_kernel, pack),
+        out_shape=(sds((width, node_dev), F32), sds((batches,), F32))
+        + tuple(sds(p.shape, F32) for p in rows),
+        in_specs=vmem(3),
+        out_specs=tuple(vmem(9)),
+        name="final",
+    )(*made)
+    new = [o.reshape(p.shape) for o, p in zip(outs[2:], params)]
+    return (outs[0].T, outs[1], *new)
 
 
 def block_loss(current, own_rows, beside_sum, neighbours, valid_part):

time: 165 us -> 107 us (0.65)
  Pallas kernels: 143 us -> 105 us
  local copies, waits for them, and re-layouts: 19 us -> 0 us
    pallas_call x8 -> x2, Pallas kernels: 143 us -> 105 us  [the longest x1 103 us: quick_body(): pl.pallas_call(functools.partial(window_kernel, owners, reps, cap, code,...]
    unnamed x37 -> x0, local copies, waits for them, and re-layouts: 12 us -> none
    reshape x6 -> x0, local copies, waits for them, and re-layouts: 3.17 us -> none  [the longest x2 1.21 us: quick_body(): gru_hidden.reshape(width, 3, width).transpose(1, 0, 2)]
    broadcast_in_dim x2 -> x0, local copies, waits for them, and re-layouts: 2.45 us -> none  [the longest x1 1.26 us: quick_body(): jnp.broadcast_to(event_times[:, None, :], (batches, 2, events))]
where the time goes in v3:
time: 107 us; the launch traced here: 106 us
  Pallas kernels  105 us (98%)
  between operations  1.31 us (1%)
    pallas_call x1, Pallas kernels, quick_body(): pl.pallas_call(functools.partial(window_kernel, owners, reps, cap, code,...  103 us
    pallas_call x1, Pallas kernels, quick_body(): pl.pallas_call(functools.partial(final_kernel, pack), out_shape=(sds((wid...  2.18 us

profile of v3, /device:TPU:0, one launch (start us, length us, event | category | flops | bytes accessed | tf_op | source)
XLA Modules:
  0.0 106.4 jit_solution(6891908618458526312)
XLA Ops:
  1.3 102.9 %window.1 = (f32[172,1024]{1,0:T(8,128)}, f32[1,128]{1,0:T(1,128)}, f32[776,128]{1,0:T(8,128)}) custom-call(s32[33,2,128]{2,1,0:T(2,128)} %bitcast.18, s32[8192]{0:T(1024)} %refs_1_.1, s32[33,2,128]{2,1,0:T(2,128)} %bitcast.19, s32[64,128]{1,0:T(8,128)} %bitcast.20, s32[2,128]{1,0:T(2,128)} %refs_4_.1, s32[2,128]{1,0:T(2,128)} %refs_5_.1, ...), custom_call_target="tpu_custom_call" | custom-call | tf_op jit(solution)/shard_map/window/pallas_call | solution.py:931
  104.2 2.2 %final.1 = (f32[172,1024]{1,0:T(8,128)}, f32[2]{0:T(128)}, f32[172,100]{1,0:T(8,128)}, f32[172,100]{1,0:T(8,128)}, f32[1,100]{1,0:T(1,128)}, /*index=5*/f32[200,...) custom-call(f32[172,1024]{1,0:T(8,128)} %get-tuple-element.21.memory_ref, ...), custom_call_target="tpu_custom_call" | custom-call | tf_op jit(solution)/shard_map/final/pallas_call | solution.py:981

commit v4 on v3

--- a/solution.py
+++ b/solution.py
@@ -609,6 +609,7 @@
         return params_ref[start : start + LANES].astype(BF)
 
     b_embed = params_ref[v : v + 1]
+    yield
     b_dec1 = params_ref[v + 1 : v + 2]
     w_dec2 = params_ref[v + 2 : v + 3]
     b_dec2 = jnp.sum(params_ref[v + 3 : v + 4])
@@ -621,6 +622,7 @@
     )
     act = jnp.tanh(direct + spread * (1.0 / neighbours) + b_embed)
     hidden = act.astype(BF)
+    yield
     h0, h1, h2 = (hidden[r * events : (r + 1) * events] for r in range(3))
     top, bottom = weight(pack.top), weight(pack.bottom)
     shared = dot(h0, top)
@@ -639,6 +641,7 @@
         g_dec2 = g_dec2 + jnp.sum(d_logit * inner, 0, keepdims=True)
         g_out = g_out + jnp.sum(d_logit, 0, keepdims=True)
         d_pre.append(jnp.where(z > 0.0, d_logit * w_dec2, 0.0))
+    yield
     g_dec1 = jnp.sum(d_pre[0] + d_pre[1], 0, keepdims=True)
     both = split2(d_pre[0] + d_pre[1])
     parts = [split2(d) for d in d_pre]
@@ -647,6 +650,7 @@
         dot_tn(h1, parts[0][0]) + dot_tn(h1, parts[0][1])
         + dot_tn(h2, parts[1][0]) + dot_tn(h2, parts[1][1])
     )
+    yield
     back = []
     for w in (top, bottom):
         back.append([(dot_nt(p[0], w) + dot_nt(p[1], w)).astype(BF) for p in parts])
@@ -656,11 +660,14 @@
     g_embed = jnp.sum(d_act, 0, keepdims=True)
     d_own = split2(d_act)
     d_nbr = split2(d_act * (1.0 / neighbours))
+    yield
     g_s = [dot_tn(x, d_own[0]) + dot_tn(x, d_own[1]) for x in (x_low, x_high)]
+    yield
     g_n = [
         dot_tn(n[0], d_nbr[0]) + dot_tn(n[0], d_nbr[1]) + dot_tn(n[1], d_nbr[0])
         for n in (n_low, n_high)
     ]
+    yield
     count = jnp.sum(valid, 0, keepdims=True)
     lane = iota((1, LANES), 1)
     scalars = jnp.where(lane == 0, g_out, jnp.where(lane == 1, loss, jnp.where(lane == 2, count, 0.0)))
@@ -768,6 +775,10 @@
 
     lax.fori_loop(1, devices, greet, 0)
     turn_memory(turned_ref, memory_ref, blocks.at[0])
+    make_lists(owners, node_dev, cap, slot_ref, nodes_ref, time_ref, lists_ref)
+    pack_bias(width, in_bias_ref, hid_bias_ref, wide, bias)
+    pack_params(pack, params, packed.at[0])
+    pack_gates(width, gru_hid_ref, [(0, width, 0)], wide, gh)
     pl.semaphore_wait(barrier, devices - 1)
 
     gathers = [
@@ -792,7 +803,6 @@
     ]
 
     gathers[0].begin()
-    make_lists(owners, node_dev, cap, slot_ref, nodes_ref, time_ref, lists_ref)
     exchange.start()
     mine.start()
 
@@ -816,9 +826,6 @@
             [(0, width, 0), (width, width, 2 * LANES), (2 * width, code, 4 * LANES)],
             wide, gi,
         ),
-        lambda: pack_gates(width, gru_hid_ref, [(0, width, 0)], wide, gh),
-        lambda: pack_bias(width, in_bias_ref, hid_bias_ref, wide, bias),
-        lambda: pack_params(pack, params, packed.at[0]),
         time_table,
         lists_in,
         codes_of(0),
@@ -854,7 +861,7 @@
         )
 
     def loss_of(b):
-        loss_step(
+        return loss_step(
             pack, b, neighbours, packed.at[b], valid_ref, own_low, own_high, nbr_low, nbr_high, flat,
             grads.at[b],
         )
@@ -868,7 +875,8 @@
     tasks = [functools.partial(rows_of, 0, i * size, size) for i in range(pieces)]
 
     def send_grads():
-        loss_of(0)
+        for _ in loss_of(0):
+            pass
         reduces[0][0].start()
 
     tasks.append(send_grads)
@@ -877,17 +885,18 @@
             tasks.pop(0)()
     for task in tasks:
         task()
+    spread(1)
+    rows_of(1, 0, events // 2)
     reduces[0][0].wait_recv()
     reduce_middle(me, grads.at[0], parts.at[0], sums.at[0], totals.at[0])
     reduces[0][1].start()
-
-    spread(1)
-    rows_of(1, 0, events)
+    rows_of(1, events // 2, events // 2)
+    partners(1)
     reduces[0][1].wait_recv()
     loss0 = update_params(pack, totals.at[0], packed.at[0], packed.at[1])
-    loss_of(1)
+    for _ in loss_of(1):
+        pass
     reduces[1][0].start()
-    partners(1)
     reduces[1][0].wait_recv()
     reduce_middle(me, grads.at[1], parts.at[1], sums.at[1], totals.at[1])
     reduces[1][1].start()

time: 107 us -> 104 us (0.972)
  Pallas kernels: 105 us -> 102 us
    pallas_call x1, Pallas kernels: 103 us -> 100 us  [quick_body(): pl.pallas_call(functools.partial(window_kernel, owners, reps, cap, code,...]
where the time goes in v4:
time: 104 us
  Pallas kernels  102 us (98%)
  between operations  1.31 us (1%)
    pallas_call x1, Pallas kernels, quick_body(): pl.pallas_call(functools.partial(window_kernel, owners, reps, cap, code,...  100 us
    pallas_call x1, Pallas kernels, quick_body(): pl.pallas_call(functools.partial(final_kernel, pack), out_shape=(sds((wid...  2.18 us

profile of v4, /device:TPU:0, one launch (start us, length us, event | category | flops | bytes accessed | tf_op | source)
XLA Modules:
  0.0 103.8 jit_solution(3392594513755708925)
XLA Ops:
  1.3 100.3 %window.1 = (f32[172,1024]{1,0:T(8,128)}, f32[1,128]{1,0:T(1,128)}, f32[776,128]{1,0:T(8,128)}) custom-call(s32[33,2,128]{2,1,0:T(2,128)} %bitcast.18, s32[8192]{0:T(1024)} %refs_1_.1, s32[33,2,128]{2,1,0:T(2,128)} %bitcast.19, s32[64,128]{1,0:T(8,128)} %bitcast.20, s32[2,128]{1,0:T(2,128)} %refs_4_.1, s32[2,128]{1,0:T(2,128)} %refs_5_.1, ...), custom_call_target="tpu_custom_call" | custom-call | tf_op jit(solution)/shard_map/window/pallas_call | solution.py:940
  101.6 2.2 %final.1 = (f32[172,1024]{1,0:T(8,128)}, f32[2]{0:T(128)}, f32[172,100]{1,0:T(8,128)}, f32[172,100]{1,0:T(8,128)}, f32[1,100]{1,0:T(1,128)}, /*index=5*/f32[200,...) custom-call(f32[172,1024]{1,0:T(8,128)} %get-tuple-element.21.memory_ref, ...), custom_call_target="tpu_custom_call" | custom-call | tf_op jit(solution)/shard_map/final/pallas_call | solution.py:990
